TPU v7x, 32 devices: a whole 2x2x4 slice. The times are simulated.
32 devices in a mesh: section: 2 (over y), rep: 4 (over z), sub: 4 (over x, core).
Axes of the slice: x: 2, y: 2, z: 4, core: 2. Of those that a mesh axis runs over, the one named last changes fastest.
Arguments:
- token_ids: int32 [8, 512], P(None, ('rep', 'sub')), may hold values from 0 to 255
- target_ids: int32 [8, 512], P(None, ('rep', 'sub')), may hold values from 0 to 255
- embedding: bfloat16 [256, 2048], P(('rep', 'sub')), may hold values from -3 to 3
- section_weight: bfloat16 [2, 2048, 2048], P('section', ('rep', 'sub')), may hold values from -0.125 to 0.125
- section_gain: float32 [2, 2048], P('section'), may hold values from 0.1 to 1.9
- final_gain: float32 [2048], replicated, may hold values from 0.5 to 1.5
Outputs:
- weight_grad: float32 [2, 2048, 2048], P('section', ('rep', 'sub'))
- gain_grad: float32 [2, 2048], P('section')
- embed_grad: float32 [256, 2048], P(('section', 'rep', 'sub'))
- final_grad: float32 [2048], replicated
All inputs are finite; a program needn't handle non-finite values.
Results may differ from a plain program's by a relative error of at most 0.024.
Values may be sent and summed in bfloat16 or wider, within the bound.
A program may use at most 64 MiB of HBM per device.

v0:
```python
import functools
import jax
import jax.numpy as jnp
from jax import lax
from jax.experimental import pallas as pl
from jax.experimental.pallas import tpu as pltpu
from jax.sharding import PartitionSpec as P

epsilon = 1e-06
gelu_coef = 0.7978845608028654
cube_coef = 0.044715


def passed_along(value, axis, steps):
    count = lax.axis_size(axis)
    initial, last = (max(0, -steps), min(count, count - steps))
    return lax.ppermute(value, axis, [(source, source + steps) for source in range(initial, last)])


def gelu(pre_act):
    return (
        0.5
        * pre_act
        * (1.0 + jnp.tanh(gelu_coef * (pre_act + cube_coef * pre_act * pre_act * pre_act)))
    )


def gelu_slope(pre_act):
    inside = gelu_coef * (pre_act + cube_coef * pre_act * pre_act * pre_act)
    tangent = jnp.tanh(inside)
    return 0.5 * (1.0 + tangent) + 0.5 * pre_act * (1.0 - tangent * tangent) * gelu_coef * (
        1.0 + 3.0 * cube_coef * pre_act * pre_act
    )


def normalize(residual, gain_row):
    values = residual.astype(jnp.float32)
    scale_inv = lax.rsqrt(jnp.mean(values * values, axis=-1, keepdims=True) + epsilon)
    normed = values * scale_inv
    return (normed, scale_inv, (normed * gain_row).astype(jnp.bfloat16))


def norm_back(grad_norm, normed, scale_inv, gain_row):
    grad_unit = grad_norm * gain_row
    grad_in = scale_inv * (
        grad_unit - normed * jnp.mean(grad_unit * normed, axis=-1, keepdims=True)
    )
    return (grad_in, jnp.sum(grad_norm * normed, axis=0))


def pick_slot(buffer, slot_index):
    return lax.dynamic_index_in_dim(buffer, slot_index, 0, keepdims=False)


def place_slot(buffer, update, slot_index):
    return lax.dynamic_update_index_in_dim(buffer, update, slot_index, 0)


def pipeline_body(token_ids, target_ids, embedding, section_weight, section_gain, final_gain):
    sections = lax.axis_size("section")
    position = lax.axis_index("section")
    micro_count = token_ids.shape[0]
    row_count = token_ids.shape[1]
    features = embedding.shape[1]
    group_size = lax.axis_size(("rep", "sub"))
    vocab_rows = embedding.shape[0] * group_size
    tick_count = micro_count + sections - 1
    contract_last = (((1,), (1,)), ((), ()))
    contract_first = (((0,), (0,)), ((), ()))
    vocab_table = lax.all_gather(embedding, ("rep", "sub"), axis=0, tiled=True)
    weight = lax.all_gather(section_weight, ("rep", "sub"), axis=1, tiled=True)[0]
    gain_row = section_gain[0]
    is_first = position == 0
    is_last = position == sections - 1
    vocab_iota = jnp.arange(vocab_rows, dtype=jnp.int32)
    onehot_in = (token_ids.reshape(-1)[:, None] == vocab_iota[None, :]).astype(jnp.bfloat16)
    embedded = jnp.dot(onehot_in, vocab_table, preferred_element_type=jnp.float32).astype(
        jnp.bfloat16
    )
    embedded = embedded.reshape(micro_count, row_count, features)
    empty_rows = jnp.zeros((row_count, features), jnp.bfloat16)
    zeros_stash = jnp.zeros((micro_count, row_count, features), jnp.bfloat16)
    zeros_pre = jnp.zeros((micro_count, row_count, features), jnp.float32)

    def forward_tick(carried, tick_index):
        arrived = carried[0]
        buffers = carried[1:]
        offset = tick_index - position
        active = (offset >= 0) & (offset < micro_count)
        slot_index = jnp.clip(offset, 0, micro_count - 1)
        residual = jnp.where(is_first, pick_slot(embedded, slot_index), arrived)

        def forward_compute(kept_activations):
            input_list, rounded_list, preactivation_list, output_list = kept_activations
            normed, scale_inv, rounded = normalize(residual, gain_row)
            pre_act = jnp.dot(rounded, weight, preferred_element_type=jnp.float32)
            returned_value = (residual.astype(jnp.float32) + gelu(pre_act)).astype(jnp.bfloat16)
            kept_activations = (
                place_slot(input_list, residual, slot_index),
                place_slot(rounded_list, rounded, slot_index),
                place_slot(preactivation_list, pre_act, slot_index),
                place_slot(output_list, returned_value, slot_index),
            )
            return (kept_activations, returned_value)

        def forward_bypass(kept_activations):
            return (kept_activations, empty_rows)

        buffers, returned_value = lax.cond(active, forward_compute, forward_bypass, buffers)
        arrived = passed_along(returned_value, "section", 1)
        return ((arrived,) + buffers, None)

    start_state = (empty_rows, zeros_stash, zeros_stash, zeros_pre, zeros_stash)
    final_state, unused_out = lax.scan(
        forward_tick, start_state, jnp.arange(tick_count, dtype=jnp.int32)
    )
    input_list, rounded_list, preactivation_list, output_list = final_state[1:]
    logit_scale = float(features) ** (-0.5)

    def head(finals):
        normed, scale_inv, final_rows = normalize(finals, final_gain)
        logits = (
            lax.dot_general(
                final_rows, vocab_table, contract_last, preferred_element_type=jnp.float32
            )
            * logit_scale
        )
        exp_logit = jnp.exp(logits)
        probability = exp_logit / jnp.sum(exp_logit, axis=-1, keepdims=True)
        onehot_out = (target_ids.reshape(-1)[:, None] == vocab_iota[None, :]).astype(jnp.float32)
        grad_logit = ((probability - onehot_out) * logit_scale).astype(jnp.bfloat16)
        embed_head = lax.dot_general(
            grad_logit, final_rows, contract_first, preferred_element_type=jnp.float32
        )
        grad_final = jnp.dot(grad_logit, vocab_table, preferred_element_type=jnp.float32)
        grad_in, final_part = norm_back(grad_final, normed, scale_inv, final_gain)
        grad_top = grad_in.astype(jnp.bfloat16).reshape(micro_count, row_count, features)
        return (embed_head, grad_top, final_part)

    def no_head(finals):
        return (
            jnp.zeros((vocab_rows, features), jnp.float32),
            zeros_stash,
            jnp.zeros((features,), jnp.float32),
        )

    embed_head, grad_top, final_part = lax.cond(
        is_last, head, no_head, output_list.reshape(-1, features)
    )

    def backward_tick(carried, tick_index):
        arrived = carried[0]
        buffers = carried[1:]
        offset = tick_index - (sections - 1 - position)
        active = (offset >= 0) & (offset < micro_count)
        slot_index = jnp.clip(offset, 0, micro_count - 1)
        grad_out = jnp.where(is_last, pick_slot(grad_top, slot_index), arrived)

        def backward_compute(kept_activations):
            preactivation_gradients, first_row_gradients, gain_accumulated = kept_activations
            grad_float = grad_out.astype(jnp.float32)
            grad_pre = (grad_float * gelu_slope(pick_slot(preactivation_list, slot_index))).astype(
                jnp.bfloat16
            )
            grad_norm = lax.dot_general(
                grad_pre, weight, contract_last, preferred_element_type=jnp.float32
            )
            normed, scale_inv, rounded = normalize(pick_slot(input_list, slot_index), gain_row)
            grad_in, gain_part = norm_back(grad_norm, normed, scale_inv, gain_row)
            sent_output = (grad_float + grad_in).astype(jnp.bfloat16)
            kept_activations = (
                place_slot(preactivation_gradients, grad_pre, slot_index),
                place_slot(first_row_gradients, sent_output, slot_index),
                gain_accumulated + gain_part,
            )
            return (kept_activations, sent_output)

        def backward_bypass(kept_activations):
            return (kept_activations, empty_rows)

        buffers, sent_output = lax.cond(active, backward_compute, backward_bypass, buffers)
        arrived = passed_along(sent_output, "section", -1)
        return ((arrived,) + buffers, None)

    back_state = (empty_rows, zeros_stash, zeros_stash, jnp.zeros((features,), jnp.float32))
    back_final, unused_back = lax.scan(
        backward_tick, back_state, jnp.arange(tick_count, dtype=jnp.int32)
    )
    preactivation_gradients, first_row_gradients, gain_accumulated = back_final[1:]
    pres_flat = preactivation_gradients.reshape(-1, features)
    rounded_flat = rounded_list.reshape(-1, features)
    weight_part = lax.psum_scatter(
        lax.dot_general(
            rounded_flat, pres_flat, contract_first, preferred_element_type=jnp.float32
        ).astype(jnp.bfloat16),
        ("rep", "sub"),
        scatter_dimension=0,
        tiled=True,
    ).astype(jnp.float32)
    gain_total = lax.psum(gain_accumulated, ("rep", "sub"))
    final_total = lax.psum(final_part, ("section", "rep", "sub"))
    embed_in = lax.dot_general(
        onehot_in,
        first_row_gradients.reshape(-1, features),
        contract_first,
        preferred_element_type=jnp.float32,
    )
    contribution = jnp.where(is_first, embed_in, 0.0) + embed_head
    embed_total = lax.psum_scatter(
        contribution, ("section", "rep", "sub"), scatter_dimension=0, tiled=True
    )
    return (weight_part[None], gain_total[None], embed_total, final_total)


row_step = 16


def add_rows(target, other, columns=None):
    @pl.loop(0, target.shape[0] // row_step)
    def _(step):
        rows = pl.ds(pl.multiple_of(step * row_step, row_step), row_step)
        extra = other[rows, :] if columns is None else other[rows, columns]
        target[rows, :] = (target[rows, :].astype(jnp.float32) + extra.astype(jnp.float32)).astype(
            target.dtype
        )


def scatter_kernel(
    reps, weight_ref, embed_ref, small_ref, weight_out, embed_out, small_out, *scratch
):
    position, rep, sub = (lax.axis_index(name) for name in ("section", "rep", "sub"))
    chip, core = sub // 2, sub % 2
    partner = {"section": position, "rep": rep, "sub": chip * 2 + 1 - core}
    across_y = {"section": 1 - position, "rep": rep, "sub": sub}
    across_x = {"section": position, "rep": rep, "sub": (1 - chip) * 2 + core}
    up = {"section": position, "rep": lax.rem(rep + 1, reps), "sub": sub}
    down = {"section": position, "rep": lax.rem(rep + reps - 1, reps), "sub": sub}
    small_sum, small_in, send_sem, recv_sem = scratch[-4:]
    tensors = []
    for index, (source, output) in enumerate(((weight_ref, weight_out), (embed_ref, embed_out))):
        tensors.append((source, output) + tuple(scratch[7 * index : 7 * index + 7]))

    barrier = pltpu.get_barrier_semaphore()
    others = [partner, across_y, across_x] + [
        {"section": position, "rep": lax.rem(rep + hop, reps), "sub": sub}
        for hop in range(1, reps)
    ]
    for other in others:
        pl.semaphore_signal(barrier, inc=1, device_id=other, device_id_type=pl.DeviceIdType.MESH)
    pl.semaphore_wait(barrier, len(others))

    counter = [0]

    def message(source, target, device):
        number = counter[0]
        counter[0] += 1
        return pltpu.make_async_remote_copy(
            src_ref=source,
            dst_ref=target,
            send_sem=send_sem.at[number],
            recv_sem=recv_sem.at[number],
            device_id=device,
            device_id_type=pl.DeviceIdType.MESH,
        )

    pending = []

    def launch(copy):
        copy.start()
        pending.append(copy)
        return copy

    rep_order = []
    for near in range((reps + 1) // 2):
        for far in (reps - 1 - near, near):
            if far not in rep_order:
                rep_order.append(far)
    kinds = ((1, 1), (1, 0), (0, 1), (0, 0))

    def towards(flip, own):
        return 1 - own if flip else own

    small_sum[0] = small_ref[...]
    small_copies = [launch(message(small_sum.at[0], small_in.at[0], partner))]

    core_copies = {}
    for flip_s, flip_x in kinds:
        for r in rep_order:
            for t, tensor in enumerate(tensors):
                s, x = towards(flip_s, position), towards(flip_x, chip)
                core_copies[flip_s, flip_x, r, t] = launch(
                    message(tensor[0].at[s, r, x, 1 - core], tensor[2].at[s, r, x], partner)
                )
    first_a, first_b = {}, {}
    for flip_s, flip_x in kinds:
        s, x = towards(flip_s, position), towards(flip_x, chip)
        for r in rep_order:
            for t, tensor in enumerate(tensors):
                source, output, held, y_a, x_a, x_b, y_b = tensor[:7]
                core_copies[flip_s, flip_x, r, t].wait_recv()
                add_rows(held.at[s, r, x], source.at[s, r, x, core])
                half = held.shape[-1] // 2
                if flip_s:
                    first_a[flip_x, r, t] = launch(
                        message(held.at[s, r, x, :, pl.ds(0, half)], y_a.at[x, r], across_y)
                    )
                if flip_x:
                    first_b[flip_s, r, t] = launch(
                        message(held.at[s, r, x, :, pl.ds(half, half)], x_b.at[s, r], across_x)
                    )
    small_copies[0].wait_recv()
    small_sum[1] = small_sum[0] + small_in[0]
    small_copies.append(launch(message(small_sum.at[1], small_in.at[1], across_y)))

    second_a, second_b = {}, {}
    for flip in (1, 0):
        for r in rep_order:
            for t, tensor in enumerate(tensors):
                source, output, held, y_a, x_a, x_b, y_b = tensor[:7]
                half = held.shape[-1] // 2
                x = towards(flip, chip)
                first_a[flip, r, t].wait_recv()
                add_rows(y_a.at[x, r], held.at[position, r, x], pl.ds(0, half))
                s = towards(flip, position)
                first_b[flip, r, t].wait_recv()
                add_rows(x_b.at[s, r], held.at[s, r, chip], pl.ds(half, half))
                if flip:
                    second_a[r, t] = launch(message(y_a.at[x, r], x_a.at[r], across_x))
                    second_b[r, t] = launch(message(x_b.at[s, r], y_b.at[r], across_y))
    small_copies[1].wait_recv()
    small_sum[2] = small_sum[1] + small_in[1]
    small_copies.append(launch(message(small_sum.at[2], small_in.at[2], across_x)))

    for r in rep_order:
        for t, tensor in enumerate(tensors):
            source, output, held, y_a, x_a, x_b, y_b = tensor[:7]
            second_a[r, t].wait_recv()
            add_rows(x_a.at[r], y_a.at[chip, r])
            second_b[r, t].wait_recv()
            add_rows(y_b.at[r], x_b.at[position, r])
    small_copies[2].wait_recv()
    small_sum[3] = small_sum[2] + small_in[2]
    small_gather = []
    for hop in range(1, reps):
        there = {"section": position, "rep": lax.rem(rep + hop, reps), "sub": sub}
        small_gather.append(launch(message(small_sum.at[3], small_in.at[2 + hop], there)))

    ends = []
    for step in range(reps - 1):
        for t, tensor in enumerate(tensors):
            x_a, y_b = tensor[4], tensor[6]
            z_up, z_down = tensor[7:9]
            for color, own in enumerate((x_a, y_b)):
                for buffer, target, device, upward in (
                    (z_up, reps - 1 - step, up, True),
                    (z_down, step, down, False),
                ):
                    at_start = rep == (0 if upward else reps - 1)
                    passes = rep < target if upward else rep > target
                    here = buffer.at[color, target]
                    fresh = message(own.at[target], here, device)
                    counter[0] -= 1
                    passed = message(here, here, device)

                    @pl.when(jnp.logical_and(jnp.logical_not(at_start), jnp.logical_or(passes, rep == target)))
                    def _():
                        passed.wait_recv()

                    @pl.when(jnp.logical_and(jnp.logical_not(at_start), passes))
                    def _():
                        add_rows(here, own.at[target])
                        passed.start()

                    @pl.when(jnp.logical_and(at_start, passes))
                    def _():
                        fresh.start()

                    ends.append((passes, passed))
    for t, tensor in enumerate(tensors):
        output, x_a, y_b = tensor[1], tensor[4], tensor[6]
        z_up, z_down = tensor[7:9]
        half = x_a.shape[-1]
        for color, own in enumerate((x_a, y_b)):

            @pl.loop(0, own.shape[1] // row_step)
            def _(step):
                rows = pl.ds(pl.multiple_of(step * row_step, row_step), row_step)
                output[rows, pl.ds(color * half, half)] = own[rep, rows, :].astype(jnp.float32)

            for buffer, edge in ((z_up, 0), (z_down, reps - 1)):

                @pl.when(rep != edge)
                def _():
                    @pl.loop(0, own.shape[1] // row_step)
                    def _(step):
                        rows = pl.ds(pl.multiple_of(step * row_step, row_step), row_step)
                        output[rows, pl.ds(color * half, half)] += buffer[color, rep, rows, :].astype(
                            jnp.float32
                        )

    for copy in small_gather:
        copy.wait_recv()
    total = small_sum[3]
    for hop in range(1, reps):
        total = total + small_in[2 + hop]
    small_out[...] = total
    for copy in pending:
        copy.wait_send()
    for passes, copy in ends:

        @pl.when(passes)
        def _():
            copy.wait_send()


def scatter_sums(weight_part, embed_part, small_part):
    sections, reps, subs = (lax.axis_size(name) for name in ("section", "rep", "sub"))
    devices = sections * reps * subs
    kinds = (sections, reps, subs // 2, 2)
    weight_rows = weight_part.shape[0] // devices
    columns = weight_part.shape[1]
    embed_rows = embed_part.shape[0] // devices
    fold = max(1, row_step // embed_rows)
    weight_in = weight_part.reshape(kinds + (weight_rows, columns))
    embed_in = embed_part.astype(jnp.bfloat16).reshape(
        kinds + (embed_rows * fold, columns // fold)
    )
    pad = (-small_part.shape[0]) % 8
    small_in = jnp.pad(small_part, ((0, pad), (0, 0)))
    scratch = []
    for rows, width in (weight_in.shape[-2:], embed_in.shape[-2:]):
        half = width // 2
        for lead in (
            (sections, reps, subs // 2, rows, width),
            (subs // 2, reps, rows, half),
            (reps, rows, half),
            (sections, reps, rows, half),
            (reps, rows, half),
            (2, reps, rows, half),
            (2, reps, rows, half),
        ):
            scratch.append(pltpu.VMEM(lead, jnp.bfloat16))
    messages = 2 * (4 * reps + 4 * reps + 2 * reps + 4 * (reps - 1)) + 2 * 4 * reps + 3 + reps
    scratch += [
        pltpu.VMEM((4,) + small_in.shape, jnp.float32),
        pltpu.VMEM((2 + reps,) + small_in.shape, jnp.float32),
        pltpu.SemaphoreType.DMA((messages,)),
        pltpu.SemaphoreType.DMA((messages,)),
    ]
    vmem = pl.BlockSpec(memory_space=pltpu.VMEM)
    weight_sum, embed_sum, small_sum = pl.pallas_call(
        functools.partial(scatter_kernel, reps),
        out_shape=(
            jax.ShapeDtypeStruct(weight_in.shape[-2:], jnp.float32),
            jax.ShapeDtypeStruct(embed_in.shape[-2:], jnp.float32),
            jax.ShapeDtypeStruct(small_in.shape, jnp.float32),
        ),
        in_specs=[vmem] * 3,
        out_specs=(vmem,) * 3,
        scratch_shapes=scratch,
        compiler_params=pltpu.CompilerParams(
            collective_id=1, has_side_effects=True, vmem_limit_bytes=60 * 1024 * 1024
        ),
        name="scatter_sums",
    )(weight_in, embed_in, small_in)
    return weight_sum, embed_sum.reshape(embed_rows, columns), small_sum[: small_part.shape[0]]


def fits_replicated(mesh, weight_shape):
    layers, rows, columns = weight_shape
    return layers * rows * columns * 2 <= 16 * 1024 * 1024


def replicated_body(token_ids, target_ids, embedding, section_weight, section_gain, final_gain):
    axes = ("section", "rep", "sub")
    sections = lax.axis_size("section")
    position = lax.axis_index("section")
    features = embedding.shape[1]
    vocab_rows = embedding.shape[0] * lax.axis_size(("rep", "sub"))
    token_count = token_ids.size // sections
    contract_last = (((1,), (1,)), ((), ()))
    contract_first = (((0,), (0,)), ((), ()))
    half = features // 2
    vocab_table = jnp.concatenate(
        [
            lax.all_gather(part, ("rep", "sub"), axis=0, tiled=True)
            for part in (embedding[:, :half], embedding[:, half:])
        ],
        axis=1,
    )
    weights = lax.all_gather(section_weight[0], axes, axis=0, tiled=True)
    weights = weights.reshape(sections, features, features)
    gains = lax.all_gather(section_gain, "section", axis=0, tiled=True)
    my_tokens = lax.dynamic_slice_in_dim(token_ids.reshape(-1), position * token_count, token_count)
    my_targets = lax.dynamic_slice_in_dim(target_ids.reshape(-1), position * token_count, token_count)
    vocab_iota = jnp.arange(vocab_rows, dtype=jnp.int32)
    onehot_in = (my_tokens[:, None] == vocab_iota[None, :]).astype(jnp.bfloat16)
    residual = jnp.dot(onehot_in, vocab_table, preferred_element_type=jnp.float32).astype(
        jnp.bfloat16
    )
    saved = []
    for layer in range(sections):
        normed, scale_inv, rounded = normalize(residual, gains[layer])
        pre_act = jnp.dot(rounded, weights[layer], preferred_element_type=jnp.float32)
        saved.append((normed, scale_inv, rounded, pre_act))
        residual = (residual.astype(jnp.float32) + gelu(pre_act)).astype(jnp.bfloat16)
    logit_scale = float(features) ** (-0.5)
    normed, scale_inv, final_rows = normalize(residual, final_gain)
    logits = (
        lax.dot_general(final_rows, vocab_table, contract_last, preferred_element_type=jnp.float32)
        * logit_scale
    )
    exp_logit = jnp.exp(logits)
    probability = exp_logit / jnp.sum(exp_logit, axis=-1, keepdims=True)
    onehot_out = (my_targets[:, None] == vocab_iota[None, :]).astype(jnp.float32)
    grad_logit = ((probability - onehot_out) * logit_scale).astype(jnp.bfloat16)
    embed_head = lax.dot_general(
        grad_logit, final_rows, contract_first, preferred_element_type=jnp.float32
    )
    grad_final = jnp.dot(grad_logit, vocab_table, preferred_element_type=jnp.float32)
    grad_in, final_part = norm_back(grad_final, normed, scale_inv, final_gain)
    grad_residual = grad_in.astype(jnp.bfloat16)
    weight_parts = []
    small_parts = [final_part]
    for layer in reversed(range(sections)):
        normed, scale_inv, rounded, pre_act = saved[layer]
        grad_float = grad_residual.astype(jnp.float32)
        grad_pre = (grad_float * gelu_slope(pre_act)).astype(jnp.bfloat16)
        weight_parts.append(
            lax.dot_general(
                rounded, grad_pre, contract_first, preferred_element_type=jnp.float32
            ).astype(jnp.bfloat16)
        )
        grad_norm = lax.dot_general(
            grad_pre, weights[layer], contract_last, preferred_element_type=jnp.float32
        )
        grad_in, gain_part = norm_back(grad_norm, normed, scale_inv, gains[layer])
        small_parts.append(gain_part)
        grad_residual = (grad_float + grad_in).astype(jnp.bfloat16)
    embed_part = embed_head + lax.dot_general(
        onehot_in, grad_residual, contract_first, preferred_element_type=jnp.float32
    )
    return finish(weight_parts[::-1], embed_part, jnp.stack(small_parts), axes, position, sections)


def finish(weight_parts, embed_part, small_part, axes, position, sections):
    weight_all = jnp.concatenate(weight_parts, axis=0)
    if sections == 2 and lax.axis_size("sub") == 4 and lax.axis_size("rep") > 1:
        weight_total, embed_total, small_total = scatter_sums(weight_all, embed_part, small_part)
        gain_total = lax.dynamic_slice_in_dim(small_total, sections - position, 1, axis=0)
        return (weight_total[None], gain_total, embed_total, small_total[0])
    weight_total = lax.psum_scatter(weight_all, axes, scatter_dimension=0, tiled=True)
    embed_total = lax.psum_scatter(embed_part, axes, scatter_dimension=0, tiled=True)
    small_total = lax.psum(small_part, axes)
    gain_total = lax.dynamic_slice_in_dim(small_total, sections - position, 1, axis=0)
    return (weight_total.astype(jnp.float32)[None], gain_total, embed_total, small_total[0])


def solution(mesh):
    in_specs = (
        P(None, ("rep", "sub")),
        P(None, ("rep", "sub")),
        P(("rep", "sub"), None),
        P("section", ("rep", "sub"), None),
        P("section", None),
        P(),
    )
    out_specs = (
        P("section", ("rep", "sub"), None),
        P("section", None),
        P(("section", "rep", "sub"), None),
        P(),
    )

    def step(*arguments):
        tokens = arguments[0].size // (mesh.shape["rep"] * mesh.shape["sub"])
        replicated = fits_replicated(mesh, arguments[3].shape) and tokens % mesh.shape["section"] == 0
        chosen = replicated_body if replicated else pipeline_body
        return jax.shard_map(
            chosen, mesh=mesh, in_specs=in_specs, out_specs=out_specs, check_vma=False
        )(*arguments)

    return step
```

profile of v0, /device:TPU:8, one launch (start us, length us, event | category | flops | bytes accessed | tf_op | source)
XLA Modules:
  0.0 429.6 jit_solution(9889521058361049683)
XLA Ops:
  7.2 0.7 all-gather.4.cloned.1.call-update
  7.9 0.8 reshape.68
  8.7 0.8 reshape.69
  9.6 4.6 %all-gather.1 = f32[2,1,2048]{2,1,0:T(1,128)S(1)} all-gather(f32[1,1,2048]{2,1,0:T(1,128)} %bitcast.38), channel_id=1, replica_groups=mesh['section'=2,'rep'=4,'sub'=4] {'section'}, dimensions={0}, use_global_device_ids=true | all-gather | bytes 24576 | tf_op jit(solution)/shard_map/all_gather | solution.py:493
  14.1 0.8 fusion.58
  14.9 21.8 %all_gather.12 = bf16[256,1024]{1,0:T(8,128)(2,1)S(1)} all-gather(bf16[16,1024]{1,0:T(8,128)(2,1)S(1)} %get-tuple-element.21), channel_id=1, replica_groups=mesh['section'=2,'rep'=4,'sub'=4] {'rep','sub'}, dimensions={0}, use_global_device_ids=true | all-gather | bytes 557056 | tf_op jit(solution)/shard_map/all_gather | solution.py:486
  36.7 22.1 %all_gather.13 = bf16[256,1024]{1,0:T(8,128)(2,1)S(1)} all-gather(bf16[16,1024]{1,0:T(8,128)(2,1)S(1)} %get-tuple-element.20), channel_id=1, replica_groups=mesh['section'=2,'rep'=4,'sub'=4] {'rep','sub'}, dimensions={0}, use_global_device_ids=true | all-gather | bytes 557056 | tf_op jit(solution)/shard_map/all_gather | solution.py:486
  59.3 71.1 %all-gather.4.cloned.1.call-done = bf16[1,4096,2048]{2,1,0:T(8,128)(2,1)} async-done(((bf16[1,128,2048]{2,1,0:T(8,128)(2,1)}), bf16[1,4096,2048]{2,1,0:T(8,128)(2,1)}) %all-gather.4.cloned.1.call-update) | async-done | bytes 16777232 | tf_op jit(solution)/shard_map/all_gather | solution.py:491
  130.4 4.6 %fusion.33 = (f32[128]{0:T(128)S(1)}, bf16[128,2048]{1,0:T(8,128)(2,1)S(1)}, f32[128,2048]{1,0:T(8,128)S(1)}) fusion(f32[128,2048]{1,0:T(8,128)S(1)} %get-tuple-element.25, bf16[1,4096,2048]{2,1,0:T(8,128)(2,1)} %all-gather.4.cloned.1.call-done, f32[2048]{0:T(1024)S(1)} %bitcast.30, f32[128]{0:T(128)S(1)} %add_rsqrt_fusion.2), kind=kOutput, calls=%fused_computation.54 | convolution fusion | flops 1077936000 | bytes 12067840 | tf_op jit(solution)/shard_map/dot_general | solution.py:504
  135.0 4.7 %fusion.21 = (f32[128]{0:T(128)S(1)}, bf16[128,2048]{1,0:T(8,128)(2,1)S(1)}, f32[128,2048]{1,0:T(8,128)S(1)}) fusion(bf16[128,2048]{1,0:T(8,128)(2,1)S(1)} %get-tuple-element.19, bf16[1,4096,2048]{2,1,0:T(8,128)(2,1)} %all-gather.4.cloned.1.call-done, f32[2048]{0:T(1024)S(1)} %bitcast.34, f32[128]{0:T(128)S(1)} %add_rsqrt_fusion.1), kind=kOutput, calls=%fused_computation.42 | convolution fusion | flops 1078460288 | bytes 11019264 | tf_op jit(solution)/shard_map/dot_general | solution.py:504
  141.5 6.0 %convolution_convert_fusion = bf16[2048,2048]{1,0:T(8,128)(2,1)} fusion(bf16[128,2048]{1,0:T(8,128)(2,1)S(1)} %get-tuple-element.19, f32[2048]{0:T(1024)S(1)} %bitcast.35, f32[128]{0:T(128)S(1)} %add_rsqrt_fusion.1, f32[128,2048]{1,0:T(8,128)S(1)} %get-tuple-element.27, bf16[128,2048]{1,0:T(8,128)(2,1)S(1)} %get-tuple-element.17, ...), kind=kOutput, calls=%fused_computation.3 | convolution fusion | flops 1086062592 | bytes 11552256 | tf_op jit(solution)/shard_map/dot_general | solution.py:530
  147.5 6.9 %fusion.32 = (f32[2048]{0:T(1024)S(1)}, f32[128]{0:T(128)S(1)}, f32[128,2048]{1,0:T(8,128)S(1)}) fusion(bf16[128,2048]{1,0:T(8,128)(2,1)S(1)} %get-tuple-element.19, f32[128]{0:T(128)S(1)} %add_rsqrt_fusion.1, f32[2048]{0:T(1024)S(1)} %bitcast.36, bf16[1,4096,2048]{2,1,0:T(8,128)(2,1)} %all-gather.4.cloned.1.call-done, ...), kind=kOutput, calls=%fused_computation.53 | convolution fusion | flops 1082652544 | bytes 12609536 | tf_op jit(solution)/shard_map/dot_general | solution.py:534
  155.0 5.8 %convolution_convert_fusion.1 = bf16[2048,2048]{1,0:T(8,128)(2,1)} fusion(f32[128,2048]{1,0:T(8,128)S(1)} %get-tuple-element.25, f32[2048]{0:T(1024)S(1)} %bitcast.31, f32[128]{0:T(128)S(1)} %add_rsqrt_fusion.2, bf16[128,2048]{1,0:T(8,128)(2,1)S(1)} %fusion.23, f32[128,2048]{1,0:T(8,128)S(1)} %get-tuple-element.26), kind=kOutput, calls=%fused_computation.4 | convolution fusion | flops 1083965440 | bytes 11018752 | tf_op jit(solution)/shard_map/dot_general | solution.py:530
  160.8 3.4 multiply_reduce_fusion
  164.2 0.7 fusion.4
  164.9 1.2 reshape.71.embed_ref
  166.1 13.7 %pad_maximum_fusion = bf16[4096,2048]{1,0:T(8,128)(2,1)} fusion(bf16[2048,2048]{1,0:T(8,128)(2,1)} %convolution_convert_fusion, bf16[2048,2048]{1,0:T(8,128)(2,1)} %convolution_convert_fusion.1), kind=kLoop, calls=%fused_computation | loop fusion | flops 33554432 | bytes 33554432 | tf_op jit(solution)/shard_map/concatenate | solution.py:547
  179.8 0.7 select_maximum_fusion.small_ref
  180.5 235.6 %scatter_sums.1 = (f32[128,2048]{1,0:T(8,128)}, f32[16,1024]{1,0:T(8,128)}, f32[8,2048]{1,0:T(8,128)}) custom-call(bf16[2,4,2,2,128,2048]{5,4,3,2,1,0:T(8,128)(2,1)} %bitcast.28, bf16[2,4,2,2,16,1024]{5,4,3,2,1,0:T(8,128)(2,1)} %reshape.71.embed_ref, f32[8,2048]{1,0:T(8,128)} %select_maximum_fusion.small_ref), custom_call_target="tpu_custom_call" | custom-call | tf_op jit(solution)/shard_map/scatter_sums/pallas_call | solution.py:451
  416.1 1.4 slice.38
  417.5 0.8 slice.37
  418.4 1.5 reshape.72
  419.9 0.6 constant_dynamic-slice_fusion
  420.5 2.3 copy.12
  (28 shorter events, 3.0 us)
Async XLA Ops:
  7.2 123.3 %all-gather.4.cloned.1.call-start = ((), (), s32[]{:S(2)}) async-start(), calls=%async_computation | async-start | bytes 17301504 | tf_op jit(solution)/shard_map/all_gather | solution.py:491
  135.0 4.8 %copy-start = (f32[2048]{0:T(1024)S(1)}, f32[2048]{0:T(1024)}, u32[]{:S(2)}) copy-start(f32[2048]{0:T(1024)} %param.11) | copy-start | bytes 24580
  147.5 13.3 %slice-start = ((s8[16777216]{0:T(1024)(128)(4,1)}), s8[4194304]{0:T(1024)(128)(4,1)S(1)}, s32[]{:S(2)}) async-start(s8[16777216]{0:T(1024)(128)(4,1)} %bitcast.43), calls=%async_computation.1 | async-start | bytes 8388608
  147.5 13.3 %slice-start.1 = ((s8[16777216]{0:T(1024)(128)(4,1)}), s8[4194304]{0:T(1024)(128)(4,1)S(1)}, s32[]{:S(2)}) async-start(s8[16777216]{0:T(1024)(128)(4,1)} %bitcast.43), calls=%async_computation.2 | async-start | bytes 8388608
  147.5 13.3 %slice-start.2 = ((s8[16777216]{0:T(1024)(128)(4,1)}), s8[4194304]{0:T(1024)(128)(4,1)S(1)}, s32[]{:S(2)}) async-start(s8[16777216]{0:T(1024)(128)(4,1)} %bitcast.43), calls=%async_computation.3 | async-start | bytes 8388608
  155.0 5.8 %slice-start.3 = ((s8[16777216]{0:T(1024)(128)(4,1)}), s8[4194304]{0:T(1024)(128)(4,1)S(1)}, s32[]{:S(2)}) async-start(s8[16777216]{0:T(1024)(128)(4,1)} %bitcast.43), calls=%async_computation.4 | async-start | bytes 8388608
Sparse Core Ops, SparseCore 0:
  10.8 119.5 all-gather.3
where the time goes:
time: 430 us
  Pallas kernels  236 us (55%)
  waiting for transfers between devices  71.8 us (17%)
  blocking collectives  48.4 us (11%)
  matrix products  34.2 us (8%)
  other arithmetic  15 us (3%)
  between operations  14.2 us (3%)
  local copies, waits for them, and re-layouts  10.4 us (2%)
    pallas_call x1, Pallas kernels, scatter_sums(): pl.pallas_call(functools.partial(scatter_kernel, reps), out_shape=(jax.Sh...  236 us
    all_gather x1, waiting for transfers between devices, replicated_body(): weights = lax.all_gather(section_weight[0], axes, axis=0, tiled=True)  71.1 us
    all_gather x2, blocking collectives, replicated_body(): lax.all_gather(part, ('rep', 'sub'), axis=0, tiled=True)  43.9 us
    concatenate x1, other arithmetic, finish(): weight_all = jnp.concatenate(weight_parts, axis=0)  13.7 us
    dot_general x2, matrix products, replicated_body(): lax.dot_general(rounded, grad_pre, contract_first, preferred_element_type...  11.8 us
    dot_general x2, matrix products, replicated_body(): lax.dot_general(grad_pre, weights[layer], contract_last, preferred_elemen...  10.3 us
    dot_general x2, matrix products, replicated_body(): jnp.dot(rounded, weights[layer], preferred_element_type=jnp.float32)  9.27 us
  transfers between devices with their start and end apart: 1, of which 1 were waited for; matrix products, arithmetic and copies ran while one was open for 1% of the time, Pallas kernels for 0%

commit v1 on v0

v1 whole, which is shorter than its diff:
```python
import functools
import jax
import jax.numpy as jnp
from jax import lax
from jax.experimental import pallas as pl
from jax.experimental.pallas import tpu as pltpu
from jax.sharding import PartitionSpec as P

epsilon = 1e-06
gelu_coef = 0.7978845608028654
cube_coef = 0.044715


def passed_along(value, axis, steps):
    count = lax.axis_size(axis)
    initial, last = (max(0, -steps), min(count, count - steps))
    return lax.ppermute(value, axis, [(source, source + steps) for source in range(initial, last)])


def gelu(pre_act):
    return (
        0.5
        * pre_act
        * (1.0 + jnp.tanh(gelu_coef * (pre_act + cube_coef * pre_act * pre_act * pre_act)))
    )


def gelu_slope(pre_act):
    inside = gelu_coef * (pre_act + cube_coef * pre_act * pre_act * pre_act)
    tangent = jnp.tanh(inside)
    return 0.5 * (1.0 + tangent) + 0.5 * pre_act * (1.0 - tangent * tangent) * gelu_coef * (
        1.0 + 3.0 * cube_coef * pre_act * pre_act
    )


def normalize(residual, gain_row):
    values = residual.astype(jnp.float32)
    scale_inv = lax.rsqrt(jnp.mean(values * values, axis=-1, keepdims=True) + epsilon)
    normed = values * scale_inv
    return (normed, scale_inv, (normed * gain_row).astype(jnp.bfloat16))


def norm_back(grad_norm, normed, scale_inv, gain_row):
    grad_unit = grad_norm * gain_row
    grad_in = scale_inv * (
        grad_unit - normed * jnp.mean(grad_unit * normed, axis=-1, keepdims=True)
    )
    return (grad_in, jnp.sum(grad_norm * normed, axis=0))


def pick_slot(buffer, slot_index):
    return lax.dynamic_index_in_dim(buffer, slot_index, 0, keepdims=False)


def place_slot(buffer, update, slot_index):
    return lax.dynamic_update_index_in_dim(buffer, update, slot_index, 0)


def pipeline_body(token_ids, target_ids, embedding, section_weight, section_gain, final_gain):
    sections = lax.axis_size("section")
    position = lax.axis_index("section")
    micro_count = token_ids.shape[0]
    row_count = token_ids.shape[1]
    features = embedding.shape[1]
    group_size = lax.axis_size(("rep", "sub"))
    vocab_rows = embedding.shape[0] * group_size
    tick_count = micro_count + sections - 1
    contract_last = (((1,), (1,)), ((), ()))
    contract_first = (((0,), (0,)), ((), ()))
    vocab_table = lax.all_gather(embedding, ("rep", "sub"), axis=0, tiled=True)
    weight = lax.all_gather(section_weight, ("rep", "sub"), axis=1, tiled=True)[0]
    gain_row = section_gain[0]
    is_first = position == 0
    is_last = position == sections - 1
    vocab_iota = jnp.arange(vocab_rows, dtype=jnp.int32)
    onehot_in = (token_ids.reshape(-1)[:, None] == vocab_iota[None, :]).astype(jnp.bfloat16)
    embedded = jnp.dot(onehot_in, vocab_table, preferred_element_type=jnp.float32).astype(
        jnp.bfloat16
    )
    embedded = embedded.reshape(micro_count, row_count, features)
    empty_rows = jnp.zeros((row_count, features), jnp.bfloat16)
    zeros_stash = jnp.zeros((micro_count, row_count, features), jnp.bfloat16)
    zeros_pre = jnp.zeros((micro_count, row_count, features), jnp.float32)

    def forward_tick(carried, tick_index):
        arrived = carried[0]
        buffers = carried[1:]
        offset = tick_index - position
        active = (offset >= 0) & (offset < micro_count)
        slot_index = jnp.clip(offset, 0, micro_count - 1)
        residual = jnp.where(is_first, pick_slot(embedded, slot_index), arrived)

        def forward_compute(kept_activations):
            input_list, rounded_list, preactivation_list, output_list = kept_activations
            normed, scale_inv, rounded = normalize(residual, gain_row)
            pre_act = jnp.dot(rounded, weight, preferred_element_type=jnp.float32)
            returned_value = (residual.astype(jnp.float32) + gelu(pre_act)).astype(jnp.bfloat16)
            kept_activations = (
                place_slot(input_list, residual, slot_index),
                place_slot(rounded_list, rounded, slot_index),
                place_slot(preactivation_list, pre_act, slot_index),
                place_slot(output_list, returned_value, slot_index),
            )
            return (kept_activations, returned_value)

        def forward_bypass(kept_activations):
            return (kept_activations, empty_rows)

        buffers, returned_value = lax.cond(active, forward_compute, forward_bypass, buffers)
        arrived = passed_along(returned_value, "section", 1)
        return ((arrived,) + buffers, None)

    start_state = (empty_rows, zeros_stash, zeros_stash, zeros_pre, zeros_stash)
    final_state, unused_out = lax.scan(
        forward_tick, start_state, jnp.arange(tick_count, dtype=jnp.int32)
    )
    input_list, rounded_list, preactivation_list, output_list = final_state[1:]
    logit_scale = float(features) ** (-0.5)

    def head(finals):
        normed, scale_inv, final_rows = normalize(finals, final_gain)
        logits = (
            lax.dot_general(
                final_rows, vocab_table, contract_last, preferred_element_type=jnp.float32
            )
            * logit_scale
        )
        exp_logit = jnp.exp(logits)
        probability = exp_logit / jnp.sum(exp_logit, axis=-1, keepdims=True)
        onehot_out = (target_ids.reshape(-1)[:, None] == vocab_iota[None, :]).astype(jnp.float32)
        grad_logit = ((probability - onehot_out) * logit_scale).astype(jnp.bfloat16)
        embed_head = lax.dot_general(
            grad_logit, final_rows, contract_first, preferred_element_type=jnp.float32
        )
        grad_final = jnp.dot(grad_logit, vocab_table, preferred_element_type=jnp.float32)
        grad_in, final_part = norm_back(grad_final, normed, scale_inv, final_gain)
        grad_top = grad_in.astype(jnp.bfloat16).reshape(micro_count, row_count, features)
        return (embed_head, grad_top, final_part)

    def no_head(finals):
        return (
            jnp.zeros((vocab_rows, features), jnp.float32),
            zeros_stash,
            jnp.zeros((features,), jnp.float32),
        )

    embed_head, grad_top, final_part = lax.cond(
        is_last, head, no_head, output_list.reshape(-1, features)
    )

    def backward_tick(carried, tick_index):
        arrived = carried[0]
        buffers = carried[1:]
        offset = tick_index - (sections - 1 - position)
        active = (offset >= 0) & (offset < micro_count)
        slot_index = jnp.clip(offset, 0, micro_count - 1)
        grad_out = jnp.where(is_last, pick_slot(grad_top, slot_index), arrived)

        def backward_compute(kept_activations):
            preactivation_gradients, first_row_gradients, gain_accumulated = kept_activations
            grad_float = grad_out.astype(jnp.float32)
            grad_pre = (grad_float * gelu_slope(pick_slot(preactivation_list, slot_index))).astype(
                jnp.bfloat16
            )
            grad_norm = lax.dot_general(
                grad_pre, weight, contract_last, preferred_element_type=jnp.float32
            )
            normed, scale_inv, rounded = normalize(pick_slot(input_list, slot_index), gain_row)
            grad_in, gain_part = norm_back(grad_norm, normed, scale_inv, gain_row)
            sent_output = (grad_float + grad_in).astype(jnp.bfloat16)
            kept_activations = (
                place_slot(preactivation_gradients, grad_pre, slot_index),
                place_slot(first_row_gradients, sent_output, slot_index),
                gain_accumulated + gain_part,
            )
            return (kept_activations, sent_output)

        def backward_bypass(kept_activations):
            return (kept_activations, empty_rows)

        buffers, sent_output = lax.cond(active, backward_compute, backward_bypass, buffers)
        arrived = passed_along(sent_output, "section", -1)
        return ((arrived,) + buffers, None)

    back_state = (empty_rows, zeros_stash, zeros_stash, jnp.zeros((features,), jnp.float32))
    back_final, unused_back = lax.scan(
        backward_tick, back_state, jnp.arange(tick_count, dtype=jnp.int32)
    )
    preactivation_gradients, first_row_gradients, gain_accumulated = back_final[1:]
    pres_flat = preactivation_gradients.reshape(-1, features)
    rounded_flat = rounded_list.reshape(-1, features)
    weight_part = lax.psum_scatter(
        lax.dot_general(
            rounded_flat, pres_flat, contract_first, preferred_element_type=jnp.float32
        ).astype(jnp.bfloat16),
        ("rep", "sub"),
        scatter_dimension=0,
        tiled=True,
    ).astype(jnp.float32)
    gain_total = lax.psum(gain_accumulated, ("rep", "sub"))
    final_total = lax.psum(final_part, ("section", "rep", "sub"))
    embed_in = lax.dot_general(
        onehot_in,
        first_row_gradients.reshape(-1, features),
        contract_first,
        preferred_element_type=jnp.float32,
    )
    contribution = jnp.where(is_first, embed_in, 0.0) + embed_head
    embed_total = lax.psum_scatter(
        contribution, ("section", "rep", "sub"), scatter_dimension=0, tiled=True
    )
    return (weight_part[None], gain_total[None], embed_total, final_total)


LANES = 128
SUBLANES = 8
MESH = pl.DeviceIdType.MESH
over_last = (((1,), (1,)), ((), ()))
over_first = (((0,), (0,)), ((), ()))


def matmul(left, right, dims=(((1,), (0,)), ((), ()))):
    return lax.dot_general(left, right, dims, preferred_element_type=jnp.float32)


def row_kernel(
    reps,
    ids_ref,
    emb_ref,
    w_ref,
    gain_ref,
    final_ref,
    weight_out,
    gain_out,
    embed_out,
    final_out,
    emb,
    ids,
    wc,
    wr,
    gains,
    counts,
    x0,
    x1,
    x2,
    normed,
    top,
    act,
    dx2,
    dx1,
    da,
    near,
    qt,
    hg,
    hg_in,
    dn0,
    dn0_in,
    g0,
    g0_in,
    part,
    part_in,
    scale,
    send_sem,
    w_recv,
    emb_recv,
    ids_recv,
    act_recv,
    wr_recv,
    misc_recv,
    dn0_recv,
    g0_recv,
):
    y, z, sub = (lax.axis_index(name) for name in ("section", "rep", "sub"))
    x, core = sub // 2, sub % 2
    chips = 4 * reps
    members = 4 * reps
    own_k = z * 4 + sub
    features = emb.shape[1]
    vocab = emb.shape[0]
    half = vocab // 2
    width = features // chips
    depth = features // members
    group = vocab // (2 * members)
    held = vocab // members
    blocks = features // LANES
    logit_scale = float(features) ** (-0.5)

    def device(dy, dz, dx, other_core=False):
        place = {"section": 1 - y if dy else y, "rep": lax.rem(z + dz, reps)}
        across = 1 - x if dx else x
        place["sub"] = across * 2 + (1 - core if other_core else core)
        return place

    partner = device(0, 0, 0, True)

    def chip_of(ya, za, xa):
        return za * 4 + xa * 2 + ya

    own_f = chip_of(y, z, x)

    def cols(index, size=width):
        return pl.ds(pl.multiple_of(index * size, size), size)

    barrier = pltpu.get_barrier_semaphore()
    count = 0
    for dy in range(2):
        for dz in range(reps):
            for dx in range(2):
                for dc in range(2):
                    if dy or dz or dx or dc:
                        pl.semaphore_signal(
                            barrier, inc=1, device_id=device(dy, dz, dx, bool(dc)), device_id_type=MESH
                        )
                        count += 1
    pl.semaphore_wait(barrier, count)

    numbers = [0]
    sent = []

    def message(source, target, recv, place):
        number = numbers[0]
        numbers[0] += 1
        return pltpu.make_async_remote_copy(
            src_ref=source,
            dst_ref=target,
            send_sem=send_sem.at[number],
            recv_sem=recv,
            device_id=place,
            device_id_type=MESH,
        )

    def send(source, target, recv, place, when=None):
        copy = message(source, target, recv, place)
        sent.append((when, copy))
        if when is None:
            copy.start()
        else:
            pl.when(when)(copy.start)

    def arrived(target, recv):
        pltpu.make_async_copy(target, target, recv).wait()

    below, above = z, reps - 1 - z
    both = jnp.minimum(below, above)
    z_near = []
    for step in range(1, reps):
        paired = step <= 2 * both
        hop = jnp.where(paired, (step + 1) // 2, step - both)
        up = jnp.where(paired, step % 2 == 1, above > below)
        z_near.append(jnp.where(up, z + hop, z - hop))

    def at(dy, za, dx, other_core=False):
        place = device(dy, 0, dx, other_core)
        place["rep"] = za
        return place

    gains[y] = gain_ref[...]
    send(gain_ref, gains.at[y], misc_recv.at[0], device(1, 0, 0))

    def weight_columns(layer):
        rows = cols(own_k, depth)
        for za in reversed(z_near + [z]):
            for dy, dx in ((1, 1), (1, 0), (0, 1), (0, 0)):
                if za is z and not dy and not dx:
                    continue
                there = chip_of(1 - y if dy else y, za, 1 - x if dx else x)
                send(
                    w_ref.at[:, cols(there)],
                    wc.at[layer, rows],
                    w_recv.at[layer * members + own_k],
                    at(dy, za, dx),
                    y == layer,
                )
        own = w_ref.at[:, cols(own_f)]
        send(own, wc.at[layer, rows], w_recv.at[layer * members + own_k], partner, y == layer)

    weight_columns(0)
    wc[y, cols(own_k, depth)] = w_ref[:, cols(own_f)]

    own_rows = cols(own_k, held)
    emb[own_rows] = emb_ref[...]
    for za in reversed(z_near):
        send(emb_ref, emb.at[own_rows], emb_recv.at[own_k], at(0, za, 0))
    send(emb_ref, emb.at[own_rows], emb_recv.at[own_k], device(0, 0, 1))
    send(emb_ref, emb.at[own_rows], emb_recv.at[own_k], partner)
    for za in z_near:
        k = za * 4 + sub
        block = emb.at[cols(k, held)]
        arrived(block, emb_recv.at[k])
        send(block, block, emb_recv.at[k], device(0, 0, 1))
        send(block, block, emb_recv.at[k], partner)
    weight_columns(1)

    keeper = core == y
    send(w_ref, wr.at[y], wr_recv.at[y], partner, keeper)
    send(w_ref, wr.at[y], wr_recv.at[y], device(1, 0, 0), jnp.logical_not(keeper))

    @pl.when(keeper)
    def _():
        wr[y] = w_ref[...]

    ids[own_k] = ids_ref[...]
    for dz in reversed(range(reps)):
        for dx in (1, 0):
            for dc in (1, 0):
                if dz or dx or dc:
                    send(ids_ref, ids.at[own_k], ids_recv.at[own_k], device(0, dz, dx, bool(dc)))

    for za in [z] + z_near:
        k = za * 4 + (1 - x) * 2 + core
        block = emb.at[cols(k, held)]
        arrived(block, emb_recv.at[k])
        send(block, block, emb_recv.at[k], partner)
    for za in [z] + z_near:
        for xa in (x, 1 - x):
            k = za * 4 + xa * 2 + 1 - core
            arrived(emb.at[cols(k, held)], emb_recv.at[k])

    def own_vocab(shape):
        index = lax.broadcasted_iota(jnp.int32, shape, 0)
        return 2 * index - (index & (group - 1)) + core * group

    pick = (
        lax.broadcasted_iota(jnp.int32, (half, vocab), 1) == own_vocab((half, vocab))
    ).astype(jnp.float32).astype(jnp.bfloat16)

    def sweep(body, start):
        return lax.fori_loop(0, blocks, lambda j, carry: body(cols(j, LANES), carry), start)

    flat = jnp.zeros((half, LANES), jnp.float32)

    def scale_inv(squares):
        mean = jnp.sum(squares, axis=-1, keepdims=True) * (1.0 / features)
        return jnp.broadcast_to(lax.rsqrt(mean + epsilon), (half, LANES))

    def mean_of(total):
        mean = jnp.sum(total, axis=-1, keepdims=True) * (1.0 / features)
        return jnp.broadcast_to(mean, (half, LANES))

    def look_up(block, squares):
        values = matmul(pick, emb[:, block])
        x0[:, block] = values.astype(jnp.bfloat16)
        return squares + values * values

    scale[0] = scale_inv(sweep(look_up, flat))
    arrived(gains.at[1 - y], misc_recv.at[0])

    def norm_into(target, source, slot, gain):
        def body(block, carry):
            unit = source[:, block].astype(jnp.float32) * scale[slot]
            target[:, block] = (unit * gain[:, block]).astype(jnp.bfloat16)
            return carry

        sweep(body, 0)

    norm_into(normed.at[0], x0, 0, gains.at[0])

    def near_rows(layer):
        rows = cols(core, half)

        @pl.when(y == layer)
        def _():
            near[rows] = normed[layer, :, cols(own_k, depth)]

        send(
            normed.at[layer, :, cols(z * 4 + x * 2 + 1 - core, depth)],
            near.at[rows],
            misc_recv.at[1],
            partner,
            y == layer,
        )

    def gather_columns(layer):
        for za in [z] + z_near:
            for dx in (0, 1):
                k = za * 4 + (1 - x if dx else x) * 2 + core
                block = wc.at[layer, cols(k, depth)]
                recv = w_recv.at[layer * members + k]
                if za is z and not dx:

                    @pl.when(y != layer)
                    def _():
                        arrived(block, recv)

                    send(block, block, recv, partner, y != layer)
                else:
                    arrived(block, recv)
                    send(block, block, recv, partner)

    def columns_ready(layer):
        for za in range(reps):
            for xa in range(2):
                k = za * 4 + xa * 2 + 1 - core
                arrived(wc.at[layer, cols(k, depth)], w_recv.at[layer * members + k])

    def spread(slot, block, f):
        recv = act_recv.at[slot * chips + f]
        for dy, dx in ((1, 1), (1, 0), (0, 1)):
            send(block, block, recv, device(dy, 0, dx))

    def gather_start(slot):
        block = act.at[slot, :, cols(own_f)]
        for za in reversed(z_near):
            send(block, block, act_recv.at[slot * chips + own_f], at(0, za, 0))
        spread(slot, block, own_f)

    def gather_forward(slot):
        for za in z_near:
            f = chip_of(y, za, x)
            block = act.at[slot, :, cols(f)]
            arrived(block, act_recv.at[slot * chips + f])
            spread(slot, block, f)

    def gather_finish(slot):
        for za in [z] + z_near:
            for dy, dx in ((1, 0), (0, 1), (1, 1)):
                f = chip_of(1 - y if dy else y, za, 1 - x if dx else x)
                arrived(act.at[slot, :, cols(f)], act_recv.at[slot * chips + f])

    def inner(pre_act):
        return jnp.tanh(gelu_coef * (pre_act + cube_coef * pre_act * pre_act * pre_act))

    def slope(pre_act):
        tangent = inner(pre_act)
        return 0.5 * (1.0 + tangent) + 0.5 * pre_act * (1.0 - tangent * tangent) * gelu_coef * (
            1.0 + 3.0 * cube_coef * pre_act * pre_act
        )

    def layer_out(target, source, pre):
        def body(block, squares):
            pre_act = pre[:, block].astype(jnp.float32)
            values = source[:, block].astype(jnp.float32) + 0.5 * pre_act * (1.0 + inner(pre_act))
            rounded = values.astype(jnp.bfloat16)
            target[:, block] = rounded
            values = rounded.astype(jnp.float32)
            return squares + values * values

        return scale_inv(sweep(body, flat))

    near_rows(0)
    gather_columns(0)
    columns_ready(0)
    act[0, :, cols(own_f)] = matmul(normed[0], wc[0]).astype(jnp.bfloat16)
    gather_start(0)
    gather_forward(0)

    gather_columns(1)

    @pl.when(keeper)
    def _():
        arrived(wr.at[1 - y], wr_recv.at[1 - y])

    send(wr.at[1 - y], wr.at[1 - y], wr_recv.at[1 - y], partner, keeper)
    for dz in range(reps):
        for dx in range(2):
            for dc in range(2):
                if dz or dx or dc:
                    k = lax.rem(z + dz, reps) * 4 + (1 - x if dx else x) * 2 + (1 - core if dc else core)
                    arrived(ids.at[k], ids_recv.at[k])

    token_rows = ids.shape[1] // 2
    counts[...] = jnp.zeros_like(counts)

    def pairs(k, carry):
        block = ids[k]
        rows = own_vocab((half, LANES))
        words = lax.broadcasted_iota(jnp.int32, (vocab, LANES), 0)
        total = counts[...]
        for r in range(token_rows):
            token = (rows == block[r : r + 1]).astype(jnp.float32).astype(jnp.bfloat16)
            target = (words == block[token_rows + r : token_rows + r + 1]).astype(jnp.float32)
            total = total + matmul(token, target.astype(jnp.bfloat16), over_last)
        counts[...] = total
        return carry

    lax.fori_loop(0, members, pairs, 0)
    columns_ready(1)
    gather_finish(0)

    scale[1] = layer_out(x1, x0, act.at[0])
    norm_into(normed.at[1], x1, 1, gains.at[1])
    act[1, :, cols(own_f)] = matmul(normed[1], wc[1]).astype(jnp.bfloat16)
    gather_start(1)
    near_rows(1)
    gather_forward(1)
    gather_finish(1)

    scale[2] = layer_out(x2, x1, act.at[1])
    norm_into(top, x2, 2, final_ref)
    raw = matmul(top[...], emb[...], over_last)
    exp_logit = jnp.exp(raw * logit_scale)
    probability = exp_logit / jnp.sum(exp_logit, axis=-1, keepdims=True)
    pair_counts = counts[...]
    row_counts = jnp.sum(pair_counts, axis=-1, keepdims=True)
    grad_logit = ((row_counts * probability - pair_counts) * logit_scale).astype(jnp.bfloat16)
    grad_wide = grad_logit.astype(jnp.float32)
    qt[...] = jnp.transpose(grad_wide).astype(jnp.bfloat16)
    final_mean = jnp.broadcast_to(
        jnp.sum(grad_wide * raw, axis=-1, keepdims=True) * (1.0 / features), (half, LANES)
    )
    mine = cols(core, half)

    def head_back(block, total):
        grad = matmul(grad_logit, emb[:, block])
        unit = x2[:, block].astype(jnp.float32) * scale[2]
        part[0, :, block] = jnp.sum(grad * unit, axis=0, keepdims=True)
        rounded = (scale[2] * (grad * final_ref[:, block] - unit * final_mean)).astype(jnp.bfloat16)
        dx2[:, block] = rounded
        pre_act = act[1, :, block].astype(jnp.float32)
        pre_grad = (rounded.astype(jnp.float32) * slope(pre_act)).astype(jnp.bfloat16)
        da[1, mine, block] = pre_grad
        return total + pre_grad.astype(jnp.float32) * pre_act

    scale[4] = mean_of(sweep(head_back, flat))

    @pl.when(core == y)
    def _():
        pass

    @pl.when(jnp.logical_not(keeper))
    def _():
        arrived(wr.at[y], wr_recv.at[y])
        arrived(wr.at[1 - y], wr_recv.at[1 - y])

    act[2, :, cols(own_f)] = matmul(da[1, mine], wr[1], over_last).astype(jnp.bfloat16)
    gather_start(2)
    send(da.at[1, mine], da.at[1, mine], misc_recv.at[2], partner, y == 1)
    send(part.at[0], part_in.at[0], misc_recv.at[3], partner)
    gather_forward(2)

    own_group = y * (2 * reps) + z * 2 + x
    for c in range(2):
        hg[c] = matmul(qt[cols(own_group, 2 * group)], top[...])[c * group : (c + 1) * group]
    send(hg.at[1 - core], hg_in, misc_recv.at[4], partner)

    def weight_grad():
        arrived(near.at[cols(1 - core, half)], misc_recv.at[1])
        chunk = 4 * LANES

        def body(j, carry):
            block = cols(j, chunk)
            weight_out[:, block] = matmul(near[...], da[y, :, block], over_first)
            return carry

        lax.fori_loop(0, features // chunk, body, 0)

    @pl.when(y == 1)
    def _():
        arrived(da.at[1, cols(1 - core, half)], misc_recv.at[2])
        weight_grad()

    gather_finish(2)

    def layer_back(block, total):
        grad = act[2, :, block].astype(jnp.float32)
        unit = x1[:, block].astype(jnp.float32) * scale[1]
        part[1, :, block] = jnp.sum(grad * unit, axis=0, keepdims=True)
        inside = scale[1] * (grad * gains[1, :, block] - unit * scale[4])
        rounded = (dx2[:, block].astype(jnp.float32) + inside).astype(jnp.bfloat16)
        dx1[:, block] = rounded
        pre_act = act[0, :, block].astype(jnp.float32)
        pre_grad = (rounded.astype(jnp.float32) * slope(pre_act)).astype(jnp.bfloat16)
        da[0, mine, block] = pre_grad
        return total + pre_grad.astype(jnp.float32) * pre_act

    scale[3] = mean_of(sweep(layer_back, flat))
    grad_norm = matmul(da[0, mine], wr[0], over_last)
    dn0[...] = grad_norm
    unit = x0[:, cols(own_f)].astype(jnp.float32) * scale[0]
    g0[...] = jnp.sum(grad_norm * unit, axis=0, keepdims=True)
    for rel in range(1, chips):
        j = lax.rem(own_group + rel, chips)
        place = {"section": j // (2 * reps), "rep": (j // 2) % reps, "sub": (j % 2) * 2 + core}
        send(dn0.at[cols(j, group)], dn0_in.at[own_f], dn0_recv.at[own_f], place)
    dn0_in[own_f] = dn0[cols(own_group, group)]
    own_slot = core * chips + own_f
    for dz in range(reps):
        for dx in range(2):
            for dc in range(2):
                place = {
                    "section": 0,
                    "rep": lax.rem(z + dz, reps),
                    "sub": (1 - x if dx else x) * 2 + (1 - core if dc else core),
                }
                itself = None if dz or dx or dc else y == 1
                send(g0, g0_in.at[own_slot], g0_recv.at[own_slot], place, itself)
    send(da.at[0, mine], da.at[0, mine], misc_recv.at[2], partner, y == 0)
    send(part.at[1], part_in.at[1], misc_recv.at[5], partner)

    @pl.when(y == 0)
    def _():
        g0_in[own_slot] = g0[...]
        arrived(da.at[0, cols(1 - core, half)], misc_recv.at[2])
        weight_grad()

    arrived(part_in.at[0], misc_recv.at[3])
    final_out[...] = part[0] + part_in[0]
    arrived(hg_in, misc_recv.at[4])
    arrived(part_in.at[1], misc_recv.at[5])

    @pl.when(y == 1)
    def _():
        gain_out[...] = part[1] + part_in[1]

    select = (
        lax.broadcasted_iota(jnp.int32, (group, half), 1)
        == lax.broadcasted_iota(jnp.int32, (group, half), 0) + own_group * group
    ).astype(jnp.float32).astype(jnp.bfloat16)
    own_group_rows = cols(own_group, group)
    row_scale = scale[0, own_group_rows]
    row_mean = scale[3, own_group_rows]

    for rel in range(1, chips):
        f = lax.rem(own_f + rel, chips)
        arrived(dn0_in.at[f], dn0_recv.at[f])

    def finish(f, carry):
        block = cols(f)
        grad = dn0_in[f]
        unit = matmul(select, x0[:, block]) * row_scale[:, :1]
        inside = row_scale[:, :1] * (grad * gains[0, :, block] - unit * row_mean[:, :1])
        total = matmul(select, dx1[:, block]) + inside
        embed_out[:, block] = total.astype(jnp.bfloat16).astype(jnp.float32) + hg[core, :, block] + hg_in[:, block]
        return carry

    lax.fori_loop(0, chips, finish, 0)

    @pl.when(y == 0)
    def _():
        for dz in range(reps):
            for dx in range(2):
                for dy in range(2):
                    for dc in range(2):
                        if dz or dx or dy or dc:
                            f = chip_of(1 - y if dy else y, lax.rem(z + dz, reps), 1 - x if dx else x)
                            slot = (1 - core if dc else core) * chips + f
                            arrived(g0_in.at[slot], g0_recv.at[slot])

        def gain_sum(f, carry):
            gain_out[:, cols(f)] = g0_in[f] + g0_in[chips + f]
            return carry

        lax.fori_loop(0, chips, gain_sum, 0)

    for when, copy in sent:
        if when is None:
            copy.wait_send()
        else:
            pl.when(when)(copy.wait_send)


def row_body(token_ids, target_ids, embedding, section_weight, section_gain, final_gain):
    reps = lax.axis_size("rep")
    members = 4 * reps
    chips = 4 * reps
    features = embedding.shape[1]
    vocab = embedding.shape[0] * members
    half = vocab // 2
    group = vocab // (2 * members)
    depth = section_weight.shape[1]
    width = features // chips
    token_rows = -(-token_ids.size // LANES)
    token_rows += (-token_rows) % (SUBLANES // 2)

    def rows_of(indices):
        flat = indices.reshape(-1)
        flat = jnp.pad(flat, (0, token_rows * LANES - flat.shape[0]), constant_values=-1)
        return flat.reshape(token_rows, LANES)

    ids = jnp.concatenate([rows_of(token_ids), rows_of(target_ids)], axis=0)
    f32, bf16 = jnp.float32, jnp.bfloat16
    messages = 400
    dma = pltpu.SemaphoreType.DMA
    scratch = [
        pltpu.VMEM((vocab, features), bf16),
        pltpu.VMEM((members,) + ids.shape, jnp.int32),
        pltpu.VMEM((2, features, width), bf16),
        pltpu.VMEM((2, width, features), bf16),
        pltpu.VMEM((2, 1, features), f32),
        pltpu.VMEM((half, vocab), f32),
        pltpu.VMEM((half, features), bf16),
        pltpu.VMEM((half, features), bf16),
        pltpu.VMEM((half, features), bf16),
        pltpu.VMEM((2, half, features), bf16),
        pltpu.VMEM((half, features), bf16),
        pltpu.VMEM((3, half, features), bf16),
        pltpu.VMEM((half, features), bf16),
        pltpu.VMEM((half, features), bf16),
        pltpu.VMEM((2, vocab, features), bf16),
        pltpu.VMEM((vocab, depth), bf16),
        pltpu.VMEM((vocab, half), bf16),
        pltpu.VMEM((2, group, features), f32),
        pltpu.VMEM((group, features), f32),
        pltpu.VMEM((half, width), f32),
        pltpu.VMEM((chips, group, width), f32),
        pltpu.VMEM((1, width), f32),
        pltpu.VMEM((2 * chips, 1, width), f32),
        pltpu.VMEM((2, 1, features), f32),
        pltpu.VMEM((2, 1, features), f32),
        pltpu.VMEM((5, half, LANES), f32),
        dma((messages,)),
        dma((2 * members,)),
        dma((members,)),
        dma((members,)),
        dma((3 * chips,)),
        dma((2,)),
        dma((6,)),
        dma((chips,)),
        dma((2 * chips,)),
    ]
    vmem = pl.BlockSpec(memory_space=pltpu.VMEM)
    weight_grad, gain_grad, embed_grad, final_grad = pl.pallas_call(
        functools.partial(row_kernel, reps),
        out_shape=(
            jax.ShapeDtypeStruct((depth, features), f32),
            jax.ShapeDtypeStruct((1, features), f32),
            jax.ShapeDtypeStruct((group, features), f32),
            jax.ShapeDtypeStruct((1, features), f32),
        ),
        in_specs=[vmem] * 5,
        out_specs=(vmem,) * 4,
        scratch_shapes=scratch,
        compiler_params=pltpu.CompilerParams(
            collective_id=1, has_side_effects=True, vmem_limit_bytes=60 * 1024 * 1024
        ),
        name="row_step",
    )(ids, embedding, section_weight[0], section_gain, final_gain[None])
    return weight_grad[None], gain_grad, embed_grad, final_grad[0]


def fits_rows(mesh, weight_shape, vocab):
    sections, reps, subs = (mesh.shape[name] for name in ("section", "rep", "sub"))
    layers, rows, features = weight_shape
    chips = 4 * reps
    group = vocab // (8 * reps)
    return (
        sections == 2
        and subs == 4
        and reps > 1
        and layers == 2
        and rows == features
        and features % (LANES * chips) == 0
        and features // chips == LANES
        and vocab % (64 * reps) == 0
        and group & (group - 1) == 0
        and vocab <= 1024
    )


def solution(mesh):
    in_specs = (
        P(None, ("rep", "sub")),
        P(None, ("rep", "sub")),
        P(("rep", "sub"), None),
        P("section", ("rep", "sub"), None),
        P("section", None),
        P(),
    )
    out_specs = (
        P("section", ("rep", "sub"), None),
        P("section", None),
        P(("section", "rep", "sub"), None),
        P(),
    )

    def step(*arguments):
        by_rows = fits_rows(mesh, arguments[3].shape, arguments[2].shape[0])
        chosen = row_body if by_rows else pipeline_body
        return jax.shard_map(
            chosen, mesh=mesh, in_specs=in_specs, out_specs=out_specs, check_vma=False
        )(*arguments)

    return step
```

time: 430 us -> 90.8 us (0.21)
  the two profiles are of different devices: /device:TPU:8 before, /device:TPU:0 now
where the time goes in v1:
time: 90.8 us; the launch traced here: 90.5 us
  Pallas kernels  84.2 us (93%)
  local copies, waits for them, and re-layouts  5.09 us (6%)
    pallas_call x1, Pallas kernels, row_body(): pl.pallas_call(functools.partial(row_kernel, reps), out_shape=(jax.ShapeD...  84.2 us
    unnamed x12, local copies, waits for them, and re-layouts  4.23 us

profile of v1, /device:TPU:0, one launch (start us, length us, event | category | flops | bytes accessed | tf_op | source)
XLA Modules:
  0.0 90.5 jit_solution(14969221777339217009)
XLA Ops:
  0.6 0.0 copy-start.3
  0.6 0.8 reshape.20
  1.4 0.0 copy-done.3
  1.4 0.1 reshape.22
  1.5 0.6 pad_add_fusion.ids_ref
  2.1 84.2 %row_step.1 = (f32[128,2048]{1,0:T(8,128)}, f32[1,2048]{1,0:T(1,128)}, f32[8,2048]{1,0:T(8,128)}, f32[1,2048]{1,0:T(1,128)}) custom-call(s32[8,128]{1,0:T(8,128)} %pad_add_fusion.ids_ref, bf16[16,2048]{1,0:T(8,128)(2,1)} %emb_ref.1, bf16[128,2048]{1,0:T(8,128)(2,1)} %bitcast.9, f32[1,2048]{1,0:T(1,128)} %gain_ref.1, f32[1,2048]{1,0:T(1,128)} %bitcast.10), custom_call_target="tpu_custom_call" | custom-call | tf_op jit(solution)/shard_map/row_step/pallas_call | solution.py:812
  86.3 0.0 copy-start.2
  86.3 0.0 copy-start
  86.3 2.3 %copy.14 = f32[1,128,2048]{2,1,0:T(8,128)} copy(f32[1,128,2048]{2,1,0:T(8,128)} %bitcast.8) | data formatting | bytes 2097152
  88.6 0.0 copy-done.2
  88.6 0.6 copy.15
  89.2 0.0 copy-done
  89.2 0.0 copy-start.1
  89.2 0.6 copy.16
  89.9 0.1 copy-done.1
  89.9 0.6 copy.17
  (1 shorter events, 0.0 us)
Async XLA Ops:
  0.6 0.8 copy-start.3
  86.3 2.4 %copy-start.2 = (f32[1,2048]{1,0:T(1,128)S(1)}, f32[1,2048]{1,0:T(1,128)}, u32[]{:S(2)}) copy-start(f32[1,2048]{1,0:T(1,128)} %get-tuple-element.19) | copy-start | bytes 24580
  86.3 2.9 %copy-start = (f32[8,2048]{1,0:T(8,128)S(1)}, f32[8,2048]{1,0:T(8,128)}, u32[]{:S(2)}) copy-start(f32[8,2048]{1,0:T(8,128)} %get-tuple-element.20) | copy-start | bytes 196612
  89.2 0.7 copy-start.1

commit v2 on v1

--- a/solution.py
+++ b/solution.py
@@ -225,15 +225,23 @@
 
 def row_kernel(
     reps,
-    ids_ref,
-    emb_ref,
+    relays,
+    token_hbm,
+    target_hbm,
+    emb_hbm,
+    w_hbm,
+    gain_hbm,
+    final_hbm,
+    near_hbm,
+    da_hbm,
+    small_hbm,
+    near,
+    da,
+    small,
+    token_ref,
+    target_ref,
     w_ref,
-    gain_ref,
     final_ref,
-    weight_out,
-    gain_out,
-    embed_out,
-    final_out,
     emb,
     ids,
     wc,
@@ -243,13 +251,12 @@
     x0,
     x1,
     x2,
-    normed,
+    scaled,
     top,
     act,
+    slopes,
     dx2,
     dx1,
-    da,
-    near,
     qt,
     hg,
     hg_in,
@@ -260,12 +267,15 @@
     part,
     part_in,
     scale,
+    base,
+    load_sem,
     send_sem,
     w_recv,
     emb_recv,
     ids_recv,
     act_recv,
     wr_recv,
+    da_recv,
     misc_recv,
     dn0_recv,
     g0_recv,
@@ -312,6 +322,19 @@
                             barrier, inc=1, device_id=device(dy, dz, dx, bool(dc)), device_id_type=MESH
                         )
                         count += 1
+    loads = []
+    for number, (source, target) in enumerate(
+        (
+            (emb_hbm, emb.at[cols(own_k, held)]),
+            (w_hbm.at[0], w_ref),
+            (gain_hbm, gains.at[y]),
+            (token_hbm, token_ref),
+            (target_hbm, target_ref),
+            (final_hbm, final_ref),
+        )
+    ):
+        loads.append(pltpu.make_async_copy(source, target, load_sem.at[number]))
+        loads[-1].start()
     pl.semaphore_wait(barrier, count)
 
     numbers = [0]
@@ -354,13 +377,10 @@
         place["rep"] = za
         return place
 
-    gains[y] = gain_ref[...]
-    send(gain_ref, gains.at[y], misc_recv.at[0], device(1, 0, 0))
-
-    def weight_columns(layer):
+    def weight_columns(layer, places, when, across=(1, 0)):
         rows = cols(own_k, depth)
-        for za in reversed(z_near + [z]):
-            for dy, dx in ((1, 1), (1, 0), (0, 1), (0, 0)):
+        for za in places:
+            for dy, dx in [(dy, dx) for dx in across for dy in (1, 0)]:
                 if za is z and not dy and not dx:
                     continue
                 there = chip_of(1 - y if dy else y, za, 1 - x if dx else x)
@@ -369,106 +389,168 @@
                     wc.at[layer, rows],
                     w_recv.at[layer * members + own_k],
                     at(dy, za, dx),
-                    y == layer,
+                    when,
                 )
-        own = w_ref.at[:, cols(own_f)]
-        send(own, wc.at[layer, rows], w_recv.at[layer * members + own_k], partner, y == layer)
-
-    weight_columns(0)
+
+    far_first = list(reversed(z_near))
+    first, second_plane = y == 0, y == 1
+
+    loads[0].wait()
+    own_rows = emb.at[cols(own_k, held)]
+    for za in reversed(z_near):
+        send(own_rows, own_rows, emb_recv.at[own_k], at(0, za, 0))
+    for there in (device(0, 0, 1), partner):
+        send(own_rows, own_rows, emb_recv.at[own_k], there)
+    loads[1].wait()
+    weight_columns(y, [z], None)
+    own = w_ref.at[:, cols(own_f)]
+    send(own, wc.at[y, cols(own_k, depth)], w_recv.at[y * members + own_k], partner)
+    loads[2].wait()
+    send(gains.at[y], gains.at[y], misc_recv.at[0], device(1, 0, 0))
+    for load in loads[3:]:
+        load.wait()
+
+    def packed(source, target, row):
+        entries = source[...].astype(jnp.float32).astype(jnp.bfloat16)
+        count, size = entries.shape
+        per_row = LANES // size
+        total = jnp.zeros((count, LANES), jnp.float32)
+        for r in range(per_row):
+            place = (
+                lax.broadcasted_iota(jnp.int32, (size, LANES), 1)
+                == lax.broadcasted_iota(jnp.int32, (size, LANES), 0) + r * size
+            ).astype(jnp.float32).astype(jnp.bfloat16)
+            choose = (
+                lax.broadcasted_iota(jnp.int32, (count, count), 1)
+                == lax.broadcasted_iota(jnp.int32, (count, count), 0) * per_row + r
+            ).astype(jnp.float32).astype(jnp.bfloat16)
+            spread_out = matmul(entries, place).astype(jnp.bfloat16)
+            total = total + matmul(choose, spread_out)
+        rows = count // per_row
+        target[row : row + rows] = total[:rows].astype(jnp.int32)
+
     wc[y, cols(own_k, depth)] = w_ref[:, cols(own_f)]
-
-    own_rows = cols(own_k, held)
-    emb[own_rows] = emb_ref[...]
-    for za in reversed(z_near):
-        send(emb_ref, emb.at[own_rows], emb_recv.at[own_k], at(0, za, 0))
-    send(emb_ref, emb.at[own_rows], emb_recv.at[own_k], device(0, 0, 1))
-    send(emb_ref, emb.at[own_rows], emb_recv.at[own_k], partner)
-    for za in z_near:
-        k = za * 4 + sub
-        block = emb.at[cols(k, held)]
-        arrived(block, emb_recv.at[k])
-        send(block, block, emb_recv.at[k], device(0, 0, 1))
-        send(block, block, emb_recv.at[k], partner)
-    weight_columns(1)
-
-    keeper = core == y
-    send(w_ref, wr.at[y], wr_recv.at[y], partner, keeper)
-    send(w_ref, wr.at[y], wr_recv.at[y], device(1, 0, 0), jnp.logical_not(keeper))
-
-    @pl.when(keeper)
-    def _():
-        wr[y] = w_ref[...]
-
-    ids[own_k] = ids_ref[...]
+    token_rows = token_ref.shape[0] * token_ref.shape[1] // LANES
+    packed(token_ref, ids.at[own_k], 0)
+    packed(target_ref, ids.at[own_k], token_rows)
+
     for dz in reversed(range(reps)):
         for dx in (1, 0):
             for dc in (1, 0):
                 if dz or dx or dc:
-                    send(ids_ref, ids.at[own_k], ids_recv.at[own_k], device(0, dz, dx, bool(dc)))
+                    send(ids.at[own_k], ids.at[own_k], ids_recv.at[own_k], device(0, dz, dx, bool(dc)))
+
+    keeper = core == y
+    other = jnp.logical_not(keeper)
+    for step, za in enumerate(z_near):
+        k = za * 4 + sub
+        block = emb.at[cols(k, held)]
+        arrived(block, emb_recv.at[k])
+        for there in (device(0, 0, 1), partner):
+            send(block, block, emb_recv.at[k], there)
+        if step == 0:
+            weight_columns(0, far_first, first, (0,))
+    weight_columns(0, far_first, first, (1,))
+
+    send(w_ref, wr.at[0], wr_recv.at[0], device(1, 0, 0), jnp.logical_and(other, first))
+    send(w_ref, wr.at[y], wr_recv.at[y], partner, keeper)
+
+    for dz in range(reps):
+        for dx in range(2):
+            for dc in range(2):
+                if dz or dx or dc:
+                    k = lax.rem(z + dz, reps) * 4 + (1 - x if dx else x) * 2 + (1 - core if dc else core)
+                    arrived(ids.at[k], ids_recv.at[k])
+
+    def own_vocab(shape):
+        index = lax.broadcasted_iota(jnp.int32, shape, 0)
+        return 2 * index - (index & (group - 1)) + core * group
+
+    counts[...] = jnp.zeros_like(counts)
+
+    def pairs(k, carry):
+        block = ids[k]
+        rows = own_vocab((half, LANES))
+        words = lax.broadcasted_iota(jnp.int32, (vocab, LANES), 0)
+
+        def onehot(index, first):
+            return jnp.concatenate(
+                [
+                    (index == block[first + r : first + r + 1]).astype(jnp.float32).astype(jnp.bfloat16)
+                    for r in range(token_rows)
+                ],
+                axis=1,
+            )
+
+        counts[...] += matmul(onehot(rows, 0), onehot(words, token_rows), over_last)
+        return carry
+
+    lax.fori_loop(0, members, pairs, 0)
 
     for za in [z] + z_near:
         k = za * 4 + (1 - x) * 2 + core
         block = emb.at[cols(k, held)]
         arrived(block, emb_recv.at[k])
         send(block, block, emb_recv.at[k], partner)
+    weight_columns(1, far_first, second_plane)
+
+    @pl.when(keeper)
+    def _():
+        wr[y] = w_ref[...]
+
     for za in [z] + z_near:
         for xa in (x, 1 - x):
             k = za * 4 + xa * 2 + 1 - core
             arrived(emb.at[cols(k, held)], emb_recv.at[k])
 
-    def own_vocab(shape):
-        index = lax.broadcasted_iota(jnp.int32, shape, 0)
-        return 2 * index - (index & (group - 1)) + core * group
-
     pick = (
         lax.broadcasted_iota(jnp.int32, (half, vocab), 1) == own_vocab((half, vocab))
     ).astype(jnp.float32).astype(jnp.bfloat16)
 
-    def sweep(body, start):
-        return lax.fori_loop(0, blocks, lambda j, carry: body(cols(j, LANES), carry), start)
+    def sweep(body, start, size=LANES):
+        for j in range(features // size):
+            start = body(pl.ds(j * size, size), start)
+        return start
 
     flat = jnp.zeros((half, LANES), jnp.float32)
 
-    def scale_inv(squares):
-        mean = jnp.sum(squares, axis=-1, keepdims=True) * (1.0 / features)
-        return jnp.broadcast_to(lax.rsqrt(mean + epsilon), (half, LANES))
+    def folded(values):
+        total = values[:, :LANES]
+        for j in range(1, values.shape[1] // LANES):
+            total = total + values[:, j * LANES : (j + 1) * LANES]
+        return total
 
     def mean_of(total):
         mean = jnp.sum(total, axis=-1, keepdims=True) * (1.0 / features)
         return jnp.broadcast_to(mean, (half, LANES))
 
+    def scale_inv(squares):
+        return lax.rsqrt(mean_of(squares) + epsilon)
+
+    arrived(gains.at[1 - y], misc_recv.at[0])
+
     def look_up(block, squares):
         values = matmul(pick, emb[:, block])
         x0[:, block] = values.astype(jnp.bfloat16)
-        return squares + values * values
-
-    scale[0] = scale_inv(sweep(look_up, flat))
-    arrived(gains.at[1 - y], misc_recv.at[0])
-
-    def norm_into(target, source, slot, gain):
-        def body(block, carry):
-            unit = source[:, block].astype(jnp.float32) * scale[slot]
-            target[:, block] = (unit * gain[:, block]).astype(jnp.bfloat16)
-            return carry
-
-        sweep(body, 0)
-
-    norm_into(normed.at[0], x0, 0, gains.at[0])
-
-    def near_rows(layer):
+        scaled[:, block] = (values * gains[0, :, block]).astype(jnp.bfloat16)
+        return squares + folded(values * values)
+
+    scale[0] = scale_inv(sweep(look_up, flat, 4 * LANES))
+
+    def near_rows(layer, source):
         rows = cols(core, half)
+
+        def rows_of(index):
+            block = cols(index, depth)
+            unit = source[:, block].astype(jnp.float32) * scale[layer]
+            return (unit * gains[layer, :, block]).astype(jnp.bfloat16)
 
         @pl.when(y == layer)
         def _():
-            near[rows] = normed[layer, :, cols(own_k, depth)]
-
-        send(
-            normed.at[layer, :, cols(z * 4 + x * 2 + 1 - core, depth)],
-            near.at[rows],
-            misc_recv.at[1],
-            partner,
-            y == layer,
-        )
+            near[rows] = rows_of(own_k)
+            base[...] = rows_of(z * 4 + x * 2 + 1 - core)
+
+        send(base, near.at[rows], misc_recv.at[1], partner, y == layer)
 
     def gather_columns(layer):
         for za in [z] + z_near:
@@ -493,186 +575,195 @@
                 k = za * 4 + xa * 2 + 1 - core
                 arrived(wc.at[layer, cols(k, depth)], w_recv.at[layer * members + k])
 
-    def spread(slot, block, f):
-        recv = act_recv.at[slot * chips + f]
-        for dy, dx in ((1, 1), (1, 0), (0, 1)):
+    def act_block(slot, f):
+        return act.at[slot, :, cols(f)], act_recv.at[slot * chips + f]
+
+    def pass_on(slot, f, places):
+        block, recv = act_block(slot, f)
+        for dy, dx in places:
             send(block, block, recv, device(dy, 0, dx))
 
+    straight = ((1, 1), (1, 0), (0, 1))
+    through = ((1, 0), (0, 1))
+    by_x, by_y = relays
+
     def gather_start(slot):
-        block = act.at[slot, :, cols(own_f)]
+        block, recv = act_block(slot, own_f)
         for za in reversed(z_near):
-            send(block, block, act_recv.at[slot * chips + own_f], at(0, za, 0))
-        spread(slot, block, own_f)
+            send(block, block, recv, at(0, za, 0))
+        pass_on(slot, own_f, through if 0 in by_x + by_y else straight)
+
+    def relay(slot, step, za):
+        if step in by_x:
+            f = chip_of(y, za, 1 - x)
+            arrived(*act_block(slot, f))
+            pass_on(slot, f, ((1, 0),))
+        if step in by_y:
+            f = chip_of(1 - y, za, x)
+            arrived(*act_block(slot, f))
+            pass_on(slot, f, ((0, 1),))
 
     def gather_forward(slot):
-        for za in z_near:
+        for step, za in enumerate(z_near):
             f = chip_of(y, za, x)
-            block = act.at[slot, :, cols(f)]
-            arrived(block, act_recv.at[slot * chips + f])
-            spread(slot, block, f)
-
-    def gather_finish(slot):
+            arrived(*act_block(slot, f))
+            pass_on(slot, f, through if step + 1 in by_x + by_y else straight)
+            relay(slot, step, z if step == 0 else z_near[step - 1])
+        relay(slot, reps - 1, z_near[-1])
+
+    def gather_use(slot, use, carry, between=None):
         for za in [z] + z_near:
+            carry = use(chip_of(y, za, x), carry)
+        step = 0
+        for place, za in enumerate([z] + z_near):
             for dy, dx in ((1, 0), (0, 1), (1, 1)):
                 f = chip_of(1 - y if dy else y, za, 1 - x if dx else x)
-                arrived(act.at[slot, :, cols(f)], act_recv.at[slot * chips + f])
-
-    def inner(pre_act):
-        return jnp.tanh(gelu_coef * (pre_act + cube_coef * pre_act * pre_act * pre_act))
-
-    def slope(pre_act):
-        tangent = inner(pre_act)
-        return 0.5 * (1.0 + tangent) + 0.5 * pre_act * (1.0 - tangent * tangent) * gelu_coef * (
-            1.0 + 3.0 * cube_coef * pre_act * pre_act
-        )
-
-    def layer_out(target, source, pre):
-        def body(block, squares):
-            pre_act = pre[:, block].astype(jnp.float32)
-            values = source[:, block].astype(jnp.float32) + 0.5 * pre_act * (1.0 + inner(pre_act))
+                if between is not None:
+                    between(step)
+                step += 1
+                waited = (place in by_x and (dy, dx) == (0, 1)) or (place in by_y and (dy, dx) == (1, 0))
+                if not waited:
+                    arrived(*act_block(slot, f))
+                carry = use(f, carry)
+        return carry
+
+    def cubic(pre_act):
+        square = pre_act * pre_act
+        tangent = jnp.tanh(gelu_coef * pre_act * (1.0 + cube_coef * square))
+        return square, tangent
+
+    def layer_out(slot, target, source, shifted, gain):
+        def body(f, squares):
+            block = cols(f)
+            pre_act = act[slot, :, block].astype(jnp.float32)
+            square, tangent = cubic(pre_act)
+            gate = 0.5 * (1.0 + tangent)
+            values = source[:, block].astype(jnp.float32) + pre_act * gate
             rounded = values.astype(jnp.bfloat16)
             target[:, block] = rounded
             values = rounded.astype(jnp.float32)
+            shifted[:, block] = (values * gain[:, block]).astype(jnp.bfloat16)
+            slopes[slot, :, block] = gate + 0.5 * pre_act * (1.0 - tangent * tangent) * gelu_coef * (
+                1.0 + 3.0 * cube_coef * square
+            )
             return squares + values * values
 
-        return scale_inv(sweep(body, flat))
-
-    near_rows(0)
+        return body
+
     gather_columns(0)
     columns_ready(0)
-    act[0, :, cols(own_f)] = matmul(normed[0], wc[0]).astype(jnp.bfloat16)
+    act[0, :, cols(own_f)] = (matmul(scaled[...], wc[0]) * scale[0][:, :width]).astype(jnp.bfloat16)
     gather_start(0)
+    near_rows(0, x0)
     gather_forward(0)
 
     gather_columns(1)
+
+    send(w_ref, wr.at[1], wr_recv.at[1], device(1, 0, 0), jnp.logical_and(other, second_plane))
+    squares = gather_use(0, layer_out(0, x1, x0, scaled, gains.at[1]), flat)
+
+    scale[1] = scale_inv(squares)
+    columns_ready(1)
+    act[1, :, cols(own_f)] = (matmul(scaled[...], wc[1]) * scale[1][:, :width]).astype(jnp.bfloat16)
+    gather_start(1)
+    near_rows(1, x1)
+    gather_forward(1)
 
     @pl.when(keeper)
     def _():
         arrived(wr.at[1 - y], wr_recv.at[1 - y])
 
     send(wr.at[1 - y], wr.at[1 - y], wr_recv.at[1 - y], partner, keeper)
-    for dz in range(reps):
-        for dx in range(2):
-            for dc in range(2):
-                if dz or dx or dc:
-                    k = lax.rem(z + dz, reps) * 4 + (1 - x if dx else x) * 2 + (1 - core if dc else core)
-                    arrived(ids.at[k], ids_recv.at[k])
-
-    token_rows = ids.shape[1] // 2
-    counts[...] = jnp.zeros_like(counts)
-
-    def pairs(k, carry):
-        block = ids[k]
-        rows = own_vocab((half, LANES))
-        words = lax.broadcasted_iota(jnp.int32, (vocab, LANES), 0)
-        total = counts[...]
-        for r in range(token_rows):
-            token = (rows == block[r : r + 1]).astype(jnp.float32).astype(jnp.bfloat16)
-            target = (words == block[token_rows + r : token_rows + r + 1]).astype(jnp.float32)
-            total = total + matmul(token, target.astype(jnp.bfloat16), over_last)
-        counts[...] = total
-        return carry
-
-    lax.fori_loop(0, members, pairs, 0)
-    columns_ready(1)
-    gather_finish(0)
-
-    scale[1] = layer_out(x1, x0, act.at[0])
-    norm_into(normed.at[1], x1, 1, gains.at[1])
-    act[1, :, cols(own_f)] = matmul(normed[1], wc[1]).astype(jnp.bfloat16)
-    gather_start(1)
-    near_rows(1)
-    gather_forward(1)
-    gather_finish(1)
-
-    scale[2] = layer_out(x2, x1, act.at[1])
-    norm_into(top, x2, 2, final_ref)
-    raw = matmul(top[...], emb[...], over_last)
+    second = layer_out(1, x2, x1, top, final_ref)
+
+    def second_use(f, carry):
+        squares, raw = carry
+        block = cols(f)
+        squares = second(f, squares)
+        return squares, raw + matmul(top[:, block], emb[:, block], over_last)
+
+    squares, raw = gather_use(1, second_use, (flat, jnp.zeros((half, vocab), jnp.float32)))
+
+    scale[2] = scale_inv(squares)
+    top_scale = scale[2][:, :1]
+    raw = raw * top_scale
     exp_logit = jnp.exp(raw * logit_scale)
     probability = exp_logit / jnp.sum(exp_logit, axis=-1, keepdims=True)
     pair_counts = counts[...]
     row_counts = jnp.sum(pair_counts, axis=-1, keepdims=True)
     grad_logit = ((row_counts * probability - pair_counts) * logit_scale).astype(jnp.bfloat16)
     grad_wide = grad_logit.astype(jnp.float32)
-    qt[...] = jnp.transpose(grad_wide).astype(jnp.bfloat16)
     final_mean = jnp.broadcast_to(
         jnp.sum(grad_wide * raw, axis=-1, keepdims=True) * (1.0 / features), (half, LANES)
     )
     mine = cols(core, half)
-
-    def head_back(block, total):
-        grad = matmul(grad_logit, emb[:, block])
-        unit = x2[:, block].astype(jnp.float32) * scale[2]
-        part[0, :, block] = jnp.sum(grad * unit, axis=0, keepdims=True)
-        rounded = (scale[2] * (grad * final_ref[:, block] - unit * final_mean)).astype(jnp.bfloat16)
-        dx2[:, block] = rounded
-        pre_act = act[1, :, block].astype(jnp.float32)
-        pre_grad = (rounded.astype(jnp.float32) * slope(pre_act)).astype(jnp.bfloat16)
-        da[1, mine, block] = pre_grad
-        return total + pre_grad.astype(jnp.float32) * pre_act
-
-    scale[4] = mean_of(sweep(head_back, flat))
-
-    @pl.when(core == y)
-    def _():
-        pass
 
     @pl.when(jnp.logical_not(keeper))
     def _():
         arrived(wr.at[y], wr_recv.at[y])
         arrived(wr.at[1 - y], wr_recv.at[1 - y])
 
-    act[2, :, cols(own_f)] = matmul(da[1, mine], wr[1], over_last).astype(jnp.bfloat16)
+    def keep(layer, block, index, values):
+        @pl.when(y == layer)
+        def _():
+            da[mine, block] = values
+
+        send(da.at[mine, block], da.at[mine, block], da_recv.at[index], partner, y == layer)
+
+    def wide(values, size):
+        return jnp.concatenate([values] * (size // LANES), axis=1)
+
+    def head_back(block, carry):
+        total, grad_in = carry
+        grad = matmul(grad_logit, emb[:, block])
+        top_wide, mean_wide = (wide(v, block.size) for v in (scale[2], final_mean))
+        unit = x2[:, block].astype(jnp.float32) * top_wide
+        part[0, :, block] = jnp.sum(grad * unit, axis=0, keepdims=True)
+        rounded = (top_wide * (grad * final_ref[:, block] - unit * mean_wide)).astype(jnp.bfloat16)
+        dx2[:, block] = rounded
+        pre_grad = (rounded.astype(jnp.float32) * slopes[1, :, block]).astype(jnp.bfloat16)
+        dx1[:, block] = pre_grad
+        total = total + folded(pre_grad.astype(jnp.float32) * act[1, :, block].astype(jnp.float32))
+        return total, grad_in + matmul(pre_grad, wr[1, :, block], over_last)
+
+    carry = (flat, jnp.zeros((half, width), jnp.float32))
+    carry = sweep(head_back, carry, 4 * LANES)
+    act[2, :, cols(own_f)] = carry[1].astype(jnp.bfloat16)
     gather_start(2)
-    send(da.at[1, mine], da.at[1, mine], misc_recv.at[2], partner, y == 1)
-    send(part.at[0], part_in.at[0], misc_recv.at[3], partner)
+    scale[4] = mean_of(carry[0])
+    send(part.at[0], part_in.at[0], misc_recv.at[2], partner)
+    for f in range(chips):
+        keep(1, pl.ds(f * width, width), f, dx1[:, f * width : (f + 1) * width])
     gather_forward(2)
 
+    qt[...] = jnp.transpose(grad_wide * top_scale).astype(jnp.bfloat16)
     own_group = y * (2 * reps) + z * 2 + x
     for c in range(2):
         hg[c] = matmul(qt[cols(own_group, 2 * group)], top[...])[c * group : (c + 1) * group]
-    send(hg.at[1 - core], hg_in, misc_recv.at[4], partner)
-
-    def weight_grad():
-        arrived(near.at[cols(1 - core, half)], misc_recv.at[1])
-        chunk = 4 * LANES
-
-        def body(j, carry):
-            block = cols(j, chunk)
-            weight_out[:, block] = matmul(near[...], da[y, :, block], over_first)
-            return carry
-
-        lax.fori_loop(0, features // chunk, body, 0)
-
-    @pl.when(y == 1)
-    def _():
-        arrived(da.at[1, cols(1 - core, half)], misc_recv.at[2])
-        weight_grad()
-
-    gather_finish(2)
-
-    def layer_back(block, total):
+    send(hg.at[1 - core], hg_in, misc_recv.at[3], partner)
+
+    def layer_back(f, carry):
+        total, grad_in = carry
+        block = cols(f)
         grad = act[2, :, block].astype(jnp.float32)
         unit = x1[:, block].astype(jnp.float32) * scale[1]
         part[1, :, block] = jnp.sum(grad * unit, axis=0, keepdims=True)
         inside = scale[1] * (grad * gains[1, :, block] - unit * scale[4])
         rounded = (dx2[:, block].astype(jnp.float32) + inside).astype(jnp.bfloat16)
         dx1[:, block] = rounded
-        pre_act = act[0, :, block].astype(jnp.float32)
-        pre_grad = (rounded.astype(jnp.float32) * slope(pre_act)).astype(jnp.bfloat16)
-        da[0, mine, block] = pre_grad
-        return total + pre_grad.astype(jnp.float32) * pre_act
-
-    scale[3] = mean_of(sweep(layer_back, flat))
-    grad_norm = matmul(da[0, mine], wr[0], over_last)
+        pre_grad = (rounded.astype(jnp.float32) * slopes[0, :, block]).astype(jnp.bfloat16)
+        keep(0, block, f, pre_grad)
+        total = total + pre_grad.astype(jnp.float32) * act[0, :, block].astype(jnp.float32)
+        return total, grad_in + matmul(pre_grad, wr[0, :, block], over_last)
+
+    total, grad_norm = gather_use(2, layer_back, (flat, jnp.zeros((half, width), jnp.float32)))
     dn0[...] = grad_norm
-    unit = x0[:, cols(own_f)].astype(jnp.float32) * scale[0]
+    unit = x0[:, cols(own_f)].astype(jnp.float32) * scale[0][:, :width]
     g0[...] = jnp.sum(grad_norm * unit, axis=0, keepdims=True)
     for rel in range(1, chips):
         j = lax.rem(own_group + rel, chips)
         place = {"section": j // (2 * reps), "rep": (j // 2) % reps, "sub": (j % 2) * 2 + core}
         send(dn0.at[cols(j, group)], dn0_in.at[own_f], dn0_recv.at[own_f], place)
-    dn0_in[own_f] = dn0[cols(own_group, group)]
     own_slot = core * chips + own_f
     for dz in range(reps):
         for dx in range(2):
@@ -684,46 +775,51 @@
                 }
                 itself = None if dz or dx or dc else y == 1
                 send(g0, g0_in.at[own_slot], g0_recv.at[own_slot], place, itself)
-    send(da.at[0, mine], da.at[0, mine], misc_recv.at[2], partner, y == 0)
-    send(part.at[1], part_in.at[1], misc_recv.at[5], partner)
+    send(part.at[1], part_in.at[1], misc_recv.at[4], partner)
+    scale[3] = mean_of(total)
+    dn0_in[own_f] = dn0[cols(own_group, group)]
 
     @pl.when(y == 0)
     def _():
         g0_in[own_slot] = g0[...]
-        arrived(da.at[0, cols(1 - core, half)], misc_recv.at[2])
-        weight_grad()
-
-    arrived(part_in.at[0], misc_recv.at[3])
-    final_out[...] = part[0] + part_in[0]
-    arrived(hg_in, misc_recv.at[4])
-    arrived(part_in.at[1], misc_recv.at[5])
-
-    @pl.when(y == 1)
-    def _():
-        gain_out[...] = part[1] + part_in[1]
 
     select = (
         lax.broadcasted_iota(jnp.int32, (group, half), 1)
         == lax.broadcasted_iota(jnp.int32, (group, half), 0) + own_group * group
     ).astype(jnp.float32).astype(jnp.bfloat16)
     own_group_rows = cols(own_group, group)
-    row_scale = scale[0, own_group_rows]
-    row_mean = scale[3, own_group_rows]
+    row_scale = scale[0, own_group_rows][:, :1]
+    row_mean = scale[3, own_group_rows][:, :1]
+    arrived(hg_in, misc_recv.at[3])
+    unit = matmul(select, x0[...]) * row_scale
+    rest = matmul(select, dx1[...]) - row_scale * unit * row_mean
+    hg[core] = hg[core] + hg_in[...] + rest
+    arrived(part_in.at[0], misc_recv.at[2])
+    arrived(part_in.at[1], misc_recv.at[4])
+    small[group + 1 : group + 2] = part[0] + part_in[0]
+
+    @pl.when(y == 1)
+    def _():
+        small[group : group + 1] = part[1] + part_in[1]
+
+    arrived(near.at[cols(1 - core, half)], misc_recv.at[1])
+    for j in range(chips):
+        block = da.at[cols(1 - core, half), pl.ds(j * width, width)]
+        arrived(block, da_recv.at[j])
+    stores = [
+        pltpu.make_async_copy(near, near_hbm, load_sem.at[0]),
+        pltpu.make_async_copy(da, da_hbm, load_sem.at[1]),
+        pltpu.make_async_copy(small, small_hbm, load_sem.at[2]),
+    ]
+    stores[0].start()
+    stores[1].start()
 
     for rel in range(1, chips):
         f = lax.rem(own_f + rel, chips)
         arrived(dn0_in.at[f], dn0_recv.at[f])
-
-    def finish(f, carry):
-        block = cols(f)
-        grad = dn0_in[f]
-        unit = matmul(select, x0[:, block]) * row_scale[:, :1]
-        inside = row_scale[:, :1] * (grad * gains[0, :, block] - unit * row_mean[:, :1])
-        total = matmul(select, dx1[:, block]) + inside
-        embed_out[:, block] = total.astype(jnp.bfloat16).astype(jnp.float32) + hg[core, :, block] + hg_in[:, block]
-        return carry
-
-    lax.fori_loop(0, chips, finish, 0)
+    for f in range(chips):
+        block = pl.ds(f * width, width)
+        small[:group, block] = hg[core, :, block] + dn0_in[f] * (row_scale * gains[0, :, block])
 
     @pl.when(y == 0)
     def _():
@@ -735,18 +831,48 @@
                             f = chip_of(1 - y if dy else y, lax.rem(z + dz, reps), 1 - x if dx else x)
                             slot = (1 - core if dc else core) * chips + f
                             arrived(g0_in.at[slot], g0_recv.at[slot])
-
-        def gain_sum(f, carry):
-            gain_out[:, cols(f)] = g0_in[f] + g0_in[chips + f]
-            return carry
-
-        lax.fori_loop(0, chips, gain_sum, 0)
-
+        for f in range(chips):
+            small[group : group + 1, f * width : (f + 1) * width] = g0_in[f] + g0_in[chips + f]
+
+    stores[2].start()
     for when, copy in sent:
         if when is None:
             copy.wait_send()
         else:
             pl.when(when)(copy.wait_send)
+    for store in stores:
+        store.wait()
+
+
+def last_kernel(
+    steps, near_hbm, da_hbm, small_hbm, weight_hbm, gain_hbm, embed_hbm, final_hbm, near, da, small, weight, sems
+):
+    group = embed_hbm.shape[0]
+    size = da.shape[1] // steps
+    blocks = [pl.ds(step * size, size) for step in range(steps)]
+    loads = [pltpu.make_async_copy(near_hbm, near, sems.at[0, steps])]
+    for step, block in enumerate(blocks):
+        loads.append(pltpu.make_async_copy(da_hbm.at[:, block], da.at[:, block], sems.at[0, step]))
+    loads.append(pltpu.make_async_copy(small_hbm, small, sems.at[0, steps + 1]))
+    for load in loads:
+        load.start()
+    loads[0].wait()
+    copies = []
+    for step, block in enumerate(blocks):
+        loads[1 + step].wait()
+        weight[:, block] = matmul(near[...], da[:, block], over_first)
+        copies.append(
+            pltpu.make_async_copy(weight.at[:, block], weight_hbm.at[:, block], sems.at[1, step])
+        )
+        copies[-1].start()
+    loads[-1].wait()
+    for row, count, target in ((0, group, embed_hbm), (group, 1, gain_hbm), (group + 1, 1, final_hbm)):
+        copies.append(
+            pltpu.make_async_copy(small.at[pl.ds(row, count)], target, sems.at[1, steps + row - group + 1 if row else steps])
+        )
+        copies[-1].start()
+    for copy in copies:
+        copy.wait()
 
 
 def row_body(token_ids, target_ids, embedding, section_weight, section_gain, final_gain):
@@ -759,21 +885,19 @@
     group = vocab // (2 * members)
     depth = section_weight.shape[1]
     width = features // chips
-    token_rows = -(-token_ids.size // LANES)
-    token_rows += (-token_rows) % (SUBLANES // 2)
-
-    def rows_of(indices):
-        flat = indices.reshape(-1)
-        flat = jnp.pad(flat, (0, token_rows * LANES - flat.shape[0]), constant_values=-1)
-        return flat.reshape(token_rows, LANES)
-
-    ids = jnp.concatenate([rows_of(token_ids), rows_of(target_ids)], axis=0)
+    token_rows = token_ids.size // LANES
     f32, bf16 = jnp.float32, jnp.bfloat16
     messages = 400
     dma = pltpu.SemaphoreType.DMA
-    scratch = [
+    small_rows = SUBLANES * (-(-(group + 2) // SUBLANES))
+    results = (((vocab, depth), bf16), ((vocab, features), bf16), ((small_rows, features), f32))
+    scratch = [pltpu.VMEM(*result) for result in results] + [
+        pltpu.VMEM(token_ids.shape, jnp.int32),
+        pltpu.VMEM(target_ids.shape, jnp.int32),
+        pltpu.VMEM((depth, features), bf16),
+        pltpu.VMEM((1, features), f32),
         pltpu.VMEM((vocab, features), bf16),
-        pltpu.VMEM((members,) + ids.shape, jnp.int32),
+        pltpu.VMEM((members, 2 * token_rows, LANES), jnp.int32),
         pltpu.VMEM((2, features, width), bf16),
         pltpu.VMEM((2, width, features), bf16),
         pltpu.VMEM((2, 1, features), f32),
@@ -781,13 +905,12 @@
         pltpu.VMEM((half, features), bf16),
         pltpu.VMEM((half, features), bf16),
         pltpu.VMEM((half, features), bf16),
-        pltpu.VMEM((2, half, features), bf16),
+        pltpu.VMEM((half, features), bf16),
         pltpu.VMEM((half, features), bf16),
         pltpu.VMEM((3, half, features), bf16),
+        pltpu.VMEM((2, half, features), f32),
         pltpu.VMEM((half, features), bf16),
         pltpu.VMEM((half, features), bf16),
-        pltpu.VMEM((2, vocab, features), bf16),
-        pltpu.VMEM((vocab, depth), bf16),
         pltpu.VMEM((vocab, half), bf16),
         pltpu.VMEM((2, group, features), f32),
         pltpu.VMEM((group, features), f32),
@@ -798,40 +921,55 @@
         pltpu.VMEM((2, 1, features), f32),
         pltpu.VMEM((2, 1, features), f32),
         pltpu.VMEM((5, half, LANES), f32),
+        pltpu.VMEM((half, depth), bf16),
+        dma((6,)),
         dma((messages,)),
         dma((2 * members,)),
         dma((members,)),
         dma((members,)),
         dma((3 * chips,)),
         dma((2,)),
-        dma((6,)),
+        dma((chips,)),
+        dma((5,)),
         dma((chips,)),
         dma((2 * chips,)),
     ]
-    vmem = pl.BlockSpec(memory_space=pltpu.VMEM)
+    hbm = pl.BlockSpec(memory_space=pltpu.HBM)
+    near, da, small = pl.pallas_call(
+        functools.partial(row_kernel, reps, ((), ())),
+        out_shape=tuple(jax.ShapeDtypeStruct(*result) for result in results),
+        in_specs=[hbm] * 6,
+        out_specs=(hbm,) * 3,
+        scratch_shapes=scratch,
+        compiler_params=pltpu.CompilerParams(
+            collective_id=1, has_side_effects=True, vmem_limit_bytes=62 * 1024 * 1024
+        ),
+        name="row_step",
+    )(token_ids, target_ids, embedding, section_weight, section_gain, final_gain[None])
+    steps = 4
     weight_grad, gain_grad, embed_grad, final_grad = pl.pallas_call(
-        functools.partial(row_kernel, reps),
+        functools.partial(last_kernel, steps),
         out_shape=(
             jax.ShapeDtypeStruct((depth, features), f32),
             jax.ShapeDtypeStruct((1, features), f32),
             jax.ShapeDtypeStruct((group, features), f32),
             jax.ShapeDtypeStruct((1, features), f32),
         ),
-        in_specs=[vmem] * 5,
-        out_specs=(vmem,) * 4,
-        scratch_shapes=scratch,
-        compiler_params=pltpu.CompilerParams(
-            collective_id=1, has_side_effects=True, vmem_limit_bytes=60 * 1024 * 1024
-        ),
-        name="row_step",
-    )(ids, embedding, section_weight[0], section_gain, final_gain[None])
+        in_specs=[hbm] * 3,
+        out_specs=(hbm,) * 4,
+        scratch_shapes=[pltpu.VMEM(*result) for result in results]
+        + [pltpu.VMEM((depth, features), f32), dma((2, steps + 3))],
+        compiler_params=pltpu.CompilerParams(vmem_limit_bytes=62 * 1024 * 1024),
+        name="last_step",
+    )(near, da, small)
     return weight_grad[None], gain_grad, embed_grad, final_grad[0]
 
 
-def fits_rows(mesh, weight_shape, vocab):
+def fits_rows(mesh, token_shape, weight_shape, vocab):
     sections, reps, subs = (mesh.shape[name] for name in ("section", "rep", "sub"))
     layers, rows, features = weight_shape
     chips = 4 * reps
+    micros, columns = token_shape[0], token_shape[1] // chips
     group = vocab // (8 * reps)
     return (
         sections == 2
@@ -843,7 +981,9 @@
         and features // chips == LANES
         and vocab % (64 * reps) == 0
         and group & (group - 1) == 0
-        and vocab <= 1024
+        and vocab <= 256
+        and LANES % columns == 0
+        and (micros * columns) % LANES == 0
     )
 
 
@@ -864,7 +1004,7 @@
     )
 
     def step(*arguments):
-        by_rows = fits_rows(mesh, arguments[3].shape, arguments[2].shape[0])
+        by_rows = fits_rows(mesh, arguments[0].shape, arguments[3].shape, arguments[2].shape[0])
         chosen = row_body if by_rows else pipeline_body
         return jax.shard_map(
             chosen, mesh=mesh, in_specs=in_specs, out_specs=out_specs, check_vma=False

time: 90.8 us -> 76.1 us (0.84)
  Pallas kernels: 84.2 us -> 75.3 us
  local copies, waits for them, and re-layouts: 5.09 us -> 0 us
    pallas_call x1 -> x2, Pallas kernels: 84.2 us -> 75.3 us  [the longest x1 72.6 us: row_body(): pl.pallas_call(functools.partial(row_kernel, reps, ((), ())), out_shape=t...]
    unnamed x12 -> x0, local copies, waits for them, and re-layouts: 4.23 us -> none
where the time goes in v2:
time: 76.1 us; the launch traced here: 75.9 us
  Pallas kernels  75.3 us (99%)
    pallas_call x1, Pallas kernels, row_body(): pl.pallas_call(functools.partial(row_kernel, reps, ((), ())), out_shape=t...  72.6 us
    pallas_call x1, Pallas kernels, row_body(): pl.pallas_call(functools.partial(last_kernel, steps), out_shape=(jax.Shap...  2.68 us

profile of v2, /device:TPU:0, one launch (start us, length us, event | category | flops | bytes accessed | tf_op | source)
XLA Modules:
  0.0 75.9 jit_solution(12385428047208152876)
XLA Ops:
  0.6 72.6 %row_step.1 = (bf16[256,128]{1,0:T(8,128)(2,1)}, bf16[256,2048]{1,0:T(8,128)(2,1)}, f32[16,2048]{1,0:T(8,128)}) custom-call(s32[8,32]{1,0:T(8,128)} %token_hbm.1, s32[8,32]{1,0:T(8,128)} %target_hbm.1, bf16[16,2048]{1,0:T(8,128)(2,1)} %emb_hbm.1, bf16[1,128,2048]{2,1,0:T(8,128)(2,1)} %w_hbm.1, f32[1,2048]{1,0:T(1,128)} %gain_hbm.1, f32[1,2048]{1,0:T(1,128)} %bitcast.3), custom_call_target="tpu_custom_call" | custom-call | tf_op jit(solution)/shard_map/row_step/pallas_call | solution.py:938
  73.3 2.7 %last_step.1 = (f32[128,2048]{1,0:T(8,128)}, f32[1,2048]{1,0:T(1,128)}, f32[8,2048]{1,0:T(8,128)}, f32[1,2048]{1,0:T(1,128)}) custom-call(bf16[256,128]{1,0:T(8,128)(2,1)} %get-tuple-element.11.near_hbm, bf16[256,2048]{1,0:T(8,128)(2,1)} %get-tuple-element.12.da_hbm, f32[16,2048]{1,0:T(8,128)} %get-tuple-element.13.small_hbm), custom_call_target="tpu_custom_call" | custom-call | tf_op jit(solution)/shard_map/last_step/pallas_call | solution.py:950
